TPU v7x, 32 devices: a whole 2x2x4 slice. The times are simulated.
32 devices in a mesh: dom: 8 (over y, x, core), sub: 4 (over z).
Axes of the slice: x: 2, y: 2, z: 4, core: 2. Of those that a mesh axis runs over, the one named last changes fastest.
Arguments:
- features: bfloat16 [32768, 602], P(('dom', 'sub')), may hold values from -6 to 6
- w_inner: bfloat16 [602, 256], replicated, may hold values from -0.25 to 0.25
- bias_inner: float32 [256], replicated, may hold values from -6 to 6
- w_outer: bfloat16 [256, 41], replicated, may hold values from -0.375 to 0.375
- bias_outer: float32 [41], replicated, may hold values from -6 to 6
- tiles: bfloat16 [256, 32, 128, 128], P(('dom', 'sub')), may hold values from -3 to 3
- tile_col: int32 [256, 32], P(('dom', 'sub')), may hold values from 0 to 39, as said below
- degrees: int32 [32768], P(('dom', 'sub')), may hold values from 1 to 32
- send_rows: int32 [32, 32, 128], P(('dom', 'sub')), may hold values from -1 to 1023, as said below
Outputs:
- logits: float32 [32768, 41], P(('dom', 'sub'))
Inputs may be any that keep to these rules, and one draw needn't show every extreme that they name: send_rows[e, p, s] is the row, among device e's 1024 vertices, that fills slot s of e's list for device p, or -1 for an unused slot; live slots come first and every list has 1 to 128 live slots; every sender has a full list, and in every draw some device receives full lists from all senders. tile_col[d * 8 + r, t] is the column block, in device d's column space, of tile t of row block r; the 32 column blocks of a row block are distinct.
All inputs are finite; a program needn't handle non-finite values.
Results may differ from a plain program's by a relative error of at most 0.0042.
Values may be sent and summed in bfloat16 or wider, within the bound.
A program may use at most 128 MiB of HBM per device.

v0:
```python
import functools

import jax
import jax.numpy as jnp
from jax import lax
from jax.experimental import pallas as pl
from jax.experimental.pallas import tpu as pltpu
from jax.sharding import PartitionSpec as P

MESH = pl.DeviceIdType.MESH
NT = (((1,), (1,)), ((), ()))


def kernel(
    n_dom, n_sub, *refs,
):
    hbm, (tiles_hbm, out), staged, refs = refs[:7], refs[7:9], refs[9:16], refs[16:]
    run(n_dom, n_sub, hbm, staged, tiles_hbm, out, *refs)


def run(
    n_dom, n_sub, hbm, staged, tiles_hbm, out, stage_sem, found, where_tile, found_sem,
    proj, out_in, got_in, acc_in, w_pad, scores, out_sc, got_sc, acc_sc, tiles,
    tile_sem, send_in, recv_in, send_sc, recv_sc,
    far_proj=None, far_lists=None, proj_send=None, proj_recv=None, lists_send=None, lists_recv=None,
):
    ft, w_inner, bias, w_outer, degrees, lists, tile_col = staged
    dom, sub = lax.axis_index("dom"), lax.axis_index("sub")
    peers = n_dom * n_sub
    hid, verts = proj.shape
    rows, per_row, blk, _ = tiles.shape
    own = verts // blk
    classes = w_outer.shape[0]

    def flip(a):
        total, bit = 0, 1
        while bit < n_dom:
            total = total + lax.rem(lax.div(dom, bit) + lax.div(a, bit), 2) * bit
            bit *= 2
        return total

    def target(k):
        return flip(lax.div(k, n_sub)), lax.rem(sub + lax.rem(k, n_sub), n_sub)

    def source(k):
        return flip(lax.div(k, n_sub)) * n_sub + lax.rem(sub + n_sub - lax.rem(k, n_sub), n_sub)

    def copy(src, dst, sends, recvs, k):
        return pltpu.make_async_remote_copy(
            src_ref=src.at[k], dst_ref=dst.at[k], send_sem=sends.at[k], recv_sem=recvs.at[k],
            device_id=target(k), device_id_type=MESH,
        )

    barrier = pltpu.get_barrier_semaphore()

    @pl.loop(1, peers)
    def _(k):
        pl.semaphore_signal(barrier, inc=1, device_id=target(k), device_id_type=MESH)

    staging = [
        pltpu.make_async_copy(src, dst, stage_sem.at[i]) for i, (src, dst) in enumerate(zip(hbm, staged))
    ]
    for each in staging:
        each.start()
    tile_copy = pltpu.make_async_copy(tiles_hbm, tiles, tile_sem)
    tile_copy.start()
    for each in staging:
        each.wait()
    inv = lax.rsqrt(degrees[...].astype(jnp.float32))
    w_t = w_inner[...].T
    wide = 2 * blk
    for v in range(0, verts, wide):
        part = jnp.dot(w_t, ft[:, v:v + wide], preferred_element_type=jnp.float32)
        proj[:, v:v + wide] = (part * inv[:, v:v + wide]).astype(proj.dtype)
    cols = tile_col[...]
    lane = lax.broadcasted_iota(jnp.int32, found.shape, 1)
    place = jnp.full(found.shape, -1, jnp.int32)
    for t in range(per_row):
        place = jnp.where(cols[:, t:t + 1] == lane, t, place)
    found[...] = place
    found_copy = pltpu.make_async_copy(found, where_tile, found_sem)
    found_copy.start()
    pl.semaphore_wait(barrier, peers - 1)

    def pick_for(first, second, table, lists):
        slots = jnp.concatenate([lists[pl.ds(first, 1), :], lists[pl.ds(second, 1), :]], axis=1)
        hot = lax.broadcasted_iota(jnp.int32, (verts, 2 * blk), 0) == slots
        hot = jnp.where(hot, 1.0, 0.0).astype(table.dtype)
        return jnp.dot(table[...], hot, preferred_element_type=jnp.float32).astype(table.dtype)

    def pick(k, table):
        index = [to_dom * n_sub + to_sub for to_dom, to_sub in (target(k), target(k + 1))]
        return pick_for(*index, table, lists)

    def deliver(table, outgoing, got, sends, recvs):
        first = pick(0, table)
        got[0] = first[:, :blk]
        outgoing[1] = first[:, blk:]
        copy(outgoing, got, sends, recvs, 1).start()

        @pl.loop(1, peers // 2)
        def _(pair):
            k = 2 * pair
            picked = pick(k, table)
            outgoing[k] = picked[:, :blk]
            outgoing[k + 1] = picked[:, blk:]
            copy(outgoing, got, sends, recvs, k).start()
            copy(outgoing, got, sends, recvs, k + 1).start()

    def add(acc, block, c0, c1, fresh):
        def tile(r, c):
            t = where_tile[r, c]
            found = tiles[r, jnp.maximum(t, 0)]
            return jnp.where(t >= 0, found, jnp.zeros_like(found))

        for r in range(0, rows, 2):
            weights = jnp.concatenate(
                [jnp.concatenate([tile(r + q, c0), tile(r + q, c1)], axis=1) for q in range(2)],
                axis=0,
            )
            term = lax.dot_general(block, weights, NT, preferred_element_type=jnp.float32)
            span = slice(r * blk, (r + 2) * blk)
            acc[:, span] = term if fresh else acc[:, span] + term

    def add_own(table, acc):
        for c in range(0, own, 2):
            add(acc, table[:, c * blk:(c + 2) * blk], c, c + 1, c == 0)

    def aggregate(table, outgoing, got, sends, recvs, acc):
        add_own(table, acc)

        def arrived(k):
            block = jnp.concatenate([got[k], got[k + 1]], axis=1)
            add(acc, block, own + source(k), own + source(k + 1), False)

        copy(outgoing, got, sends, recvs, 1).wait_recv()
        arrived(0)

        @pl.loop(1, peers // 2)
        def _(pair):
            k = 2 * pair
            copy(outgoing, got, sends, recvs, k).wait_recv()
            copy(outgoing, got, sends, recvs, k + 1).wait_recv()
            arrived(k)

    relay = far_proj is not None
    if relay:
        half = lax.div(sub, 2)
        sibling, near, far = 1 + 4 * half - sub, 2 - half, 3 - 3 * half
        middle = sub == 1 + half
        mine = dom * n_sub + sub
        per_step = 2 * n_dom
        direct = 2

        def to_slot(j, source_index, to_dom, to_sub):
            return pltpu.make_async_remote_copy(
                src_ref=out_in.at[j], dst_ref=got_in.at[source_index], send_sem=send_in.at[j],
                recv_sem=recv_in.at[source_index], device_id=(to_dom, to_sub), device_id_type=MESH,
            )

        def block_copies(slot):
            return [
                pltpu.make_async_remote_copy(
                    src_ref=src, dst_ref=dst.at[slot], send_sem=sent, recv_sem=came.at[slot],
                    device_id=(dom, near), device_id_type=MESH,
                )
                for src, dst, sent, came in (
                    (proj, far_proj, proj_send, proj_recv), (lists, far_lists, lists_send, lists_recv)
                )
            ]

        def send_block(slot):
            for each in block_copies(slot):
                each.start()

        def hand_out(table, lists, source_index, base, skip):
            def picked_for(a):
                row = flip(a) * n_sub
                return pick_for(row + sub, row + sibling, table, lists)

            first = picked_for(0)
            got_in[source_index] = first[:, :blk]
            if skip == 0:
                out_in[base + 1] = first[:, blk:]
                to_slot(base + 1, source_index, dom, sibling).start()
            for a in range(1, skip):
                out_in[base + 2 * a] = picked_for(a)[:, :blk]
                to_slot(base + 2 * a, source_index, flip(a), sub).start()

            @pl.loop(max(1, skip), n_dom)
            def _(a):
                picked = picked_for(a)
                j = base + 2 * a
                out_in[j] = picked[:, :blk]
                out_in[j + 1] = picked[:, blk:]
                to_slot(j + 1, source_index, flip(a), sibling).start()
                to_slot(j, source_index, flip(a), sub).start()

        def relay_block(slot, from_sub):
            for each in block_copies(slot):
                each.wait_recv()
            hand_out(
                far_proj.at[slot], far_lists.at[slot], dom * n_sub + from_sub, (slot + 1) * per_step,
                direct,
            )

        def send_direct():
            rows_for = [flip(a) * n_sub + far for a in range(2)]
            picked = pick_for(*rows_for, proj, lists)
            for a in range(2):
                j = per_step + 2 * a + 1
                out_in[j] = picked[:, a * blk:(a + 1) * blk]
                to_slot(j, mine, flip(a), far).start()

        def wait_for(index):
            to_slot(0, index, dom, sibling).wait_recv()

        def add_pair(e0, e1):
            block = jnp.concatenate([got_in[e0], got_in[e1]], axis=1)
            add(acc_in, block, own + e0, own + e1, False)

        pl.when(middle)(lambda: send_block(0))
        hand_out(proj, lists, mine, 0, 0)
        pl.when(jnp.logical_not(middle))(lambda: send_block(1))
        send_direct()
    else:
        deliver(proj, out_in, got_in, send_in, recv_in)
    w_pad[...] = jnp.zeros_like(w_pad)
    w_pad[0:classes, :] = w_outer[...]
    bias_col = jnp.broadcast_to(bias[...], (blk, hid)).T
    tile_copy.wait()
    found_copy.wait()
    if relay:
        add_own(proj, acc_in)
        pl.when(middle)(lambda: relay_block(0, near))
        wait_for(dom * n_sub + sibling)
        add_pair(mine, dom * n_sub + sibling)

        @pl.loop(1, n_dom)
        def _(a):
            row = flip(a) * n_sub
            wait_for(row + sub)
            wait_for(row + sibling)
            add_pair(row + sub, row + sibling)

        pl.when(middle)(lambda: relay_block(1, far))
        for plane in (near, far):
            @pl.when(jnp.logical_not(middle))
            def _():
                wait_for(dom * n_sub + plane)

            wait_for(flip(1) * n_sub + plane)
            add_pair(dom * n_sub + plane, flip(1) * n_sub + plane)

            @pl.loop(1, n_dom // 2)
            def _(pair):
                e0, e1 = flip(2 * pair) * n_sub + plane, flip(2 * pair + 1) * n_sub + plane
                wait_for(e0)
                wait_for(e1)
                add_pair(e0, e1)
    else:
        aggregate(proj, out_in, got_in, send_in, recv_in, acc_in)
    for v in range(0, verts, blk):
        span = slice(v, v + blk)
        scale = inv[:, span]
        hidden = scale * jnp.maximum(scale * acc_in[:, span] + bias_col, 0.0)
        scores[:, span] = jnp.dot(
            w_pad[...], hidden.astype(jnp.bfloat16), preferred_element_type=jnp.float32
        ).astype(scores.dtype)
    deliver(scores, out_sc, got_sc, send_sc, recv_sc)
    aggregate(scores, out_sc, got_sc, send_sc, recv_sc, acc_sc)
    out[...] = acc_sc[0:classes, :]

    @pl.loop(1, peers)
    def _(k):
        copy(out_sc, got_sc, send_sc, recv_sc, k).wait_send()

    if relay:
        for each in block_copies(0):
            each.wait_send()

        @pl.loop(1, per_step)
        def _(j):
            to_slot(j, 0, dom, sibling).wait_send()

        for a in range(direct):
            to_slot(per_step + 2 * a + 1, 0, dom, sibling).wait_send()

        @pl.when(middle)
        def _():
            for base in (per_step, 2 * per_step):
                for a in range(1, direct):
                    to_slot(base + 2 * a, 0, dom, sibling).wait_send()

            @pl.loop(2 * direct, per_step)
            def _(j):
                to_slot(per_step + j, 0, dom, sibling).wait_send()
                to_slot(2 * per_step + j, 0, dom, sibling).wait_send()
    else:
        @pl.loop(1, peers)
        def _(k):
            copy(out_in, got_in, send_in, recv_in, k).wait_send()


def on_device(
    n_dom, n_sub,
    features, w_inner, bias_inner, w_outer, bias_outer, tiles, tile_col, degrees, send_rows
):
    peers = n_dom * n_sub
    verts, hid = features.shape[0], w_inner.shape[1]
    classes = w_outer.shape[1]
    padded = 16 * ((classes + 15) // 16)
    blk = tiles.shape[2]
    columns = verts // blk + peers
    lanes = 128 * ((columns + 127) // 128)
    small = (
        features.T, w_inner, bias_inner[None, :], w_outer.T, degrees[None, :], send_rows[0], tile_col
    )
    relay = n_sub == 4
    lists_out = 6 * n_dom if relay else peers
    vmem = pl.BlockSpec(memory_space=pltpu.VMEM)
    bf16, f32 = jnp.bfloat16, jnp.float32
    agg = pl.pallas_call(
        functools.partial(kernel, n_dom, n_sub),
        out_shape=jax.ShapeDtypeStruct((classes, verts), f32),
        in_specs=[pl.BlockSpec(memory_space=pl.ANY)] * 8,
        out_specs=vmem,
        scratch_shapes=[pltpu.VMEM(each.shape, each.dtype) for each in small]
        + [
            pltpu.SemaphoreType.DMA((7,)),
            pltpu.VMEM((tiles.shape[0], lanes), jnp.int32),
            pltpu.SMEM((tiles.shape[0], lanes), jnp.int32),
            pltpu.SemaphoreType.DMA,
            pltpu.VMEM((hid, verts), bf16),
            pltpu.VMEM((lists_out, hid, blk), bf16),
            pltpu.VMEM((peers, hid, blk), bf16),
            pltpu.VMEM((hid, verts), f32),
            pltpu.VMEM((padded, hid), bf16),
            pltpu.VMEM((padded, verts), bf16),
            pltpu.VMEM((peers, padded, blk), bf16),
            pltpu.VMEM((peers, padded, blk), bf16),
            pltpu.VMEM((padded, verts), f32),
            pltpu.VMEM(tiles.shape, bf16),
            pltpu.SemaphoreType.DMA,
            pltpu.SemaphoreType.DMA((lists_out,)),
            pltpu.SemaphoreType.DMA((peers,)),
            pltpu.SemaphoreType.DMA((peers,)),
            pltpu.SemaphoreType.DMA((peers,)),
        ]
        + (
            [
                pltpu.VMEM((2, hid, verts), bf16),
                pltpu.VMEM((2, peers, blk), jnp.int32),
                pltpu.SemaphoreType.DMA,
                pltpu.SemaphoreType.DMA((2,)),
                pltpu.SemaphoreType.DMA,
                pltpu.SemaphoreType.DMA((2,)),
            ]
            if relay
            else []
        ),
        compiler_params=pltpu.CompilerParams(
            collective_id=0, has_side_effects=True, vmem_limit_bytes=56 * 1024 * 1024
        ),
    )(*small, tiles)
    inv_sqrt = lax.rsqrt(degrees.astype(f32))[:, None]
    return inv_sqrt * agg.T + bias_outer


def solution(mesh):
    return jax.shard_map(
        functools.partial(on_device, mesh.shape["dom"], mesh.shape["sub"]),
        mesh=mesh,
        in_specs=(
            P(("dom", "sub"), None),
            P(),
            P(),
            P(),
            P(),
            P(("dom", "sub"), None, None, None),
            P(("dom", "sub"), None),
            P(("dom", "sub")),
            P(("dom", "sub"), None, None),
        ),
        out_specs=P(("dom", "sub"), None),
        check_vma=False,
    )
```

profile of v0, /device:TPU:0, one launch (start us, length us, event | category | flops | bytes accessed | tf_op | source)
XLA Modules:
  0.0 65.9 jit_solution(13985689865801838480)
XLA Ops:
  0.0 0.0 copy-start
  0.0 0.7 %convert_rsqrt_fusion = f32[1024]{0:T(1024)S(1)} fusion(s32[1024]{0:T(1024)} %param.16), kind=kLoop, calls=%fused_computation.1 | loop fusion | flops 1024 | bytes 8192 | tf_op jit(solution)/shard_map/rsqrt | solution.py:366
  0.7 63.5 %shard_map.91 = f32[41,1024]{1,0:T(8,128)} custom-call(bf16[602,1024]{1,0:T(8,128)(2,1)} %bitcast.7, bf16[602,256]{1,0:T(8,128)(2,1)} %refs_1_.1, f32[1,256]{1,0:T(1,128)} %bitcast.11, bf16[41,256]{1,0:T(8,128)(2,1)} %bitcast.8, s32[1,1024]{1,0:T(1,128)} %bitcast.10, s32[32,128]{1,0:T(8,128)} %bitcast.9, s32[8,32]{1,0:T(8,128)} %refs_6_.1, ...), custom_call_target="tpu_custom_call" | custom-call | tf_op jit(solution)/shard_map/pallas_call | solution.py:323
  64.2 0.0 copy-done
  64.2 1.7 %add_bitcast_fusion = f32[1024,41]{0,1:T(8,128)} fusion(f32[41,1024]{1,0:T(8,128)} %shard_map.91, f32[41]{0:T(128)S(1)} %copy-done, f32[1024]{0:T(1024)S(1)} %convert_rsqrt_fusion), kind=kLoop, calls=%fused_computation | loop fusion | flops 83968 | bytes 340132 | tf_op jit(solution)/shard_map/add | solution.py:367
Async XLA Ops:
  0.0 64.2 %copy-start = (f32[41]{0:T(128)S(1)}, f32[41]{0:T(128)}, u32[]{:S(2)}) copy-start(f32[41]{0:T(128)} %param.13) | copy-start | bytes 496
where the time goes:
time: 66.1 us; the launch traced here: 65.9 us
  Pallas kernels  63.5 us (96%)
  other arithmetic  2.39 us (4%)
    pallas_call x1, Pallas kernels, on_device(): pl.pallas_call(functools.partial(kernel, n_dom, n_sub), out_shape=jax.Sha...  63.5 us
    add x1, other arithmetic, on_device(): return inv_sqrt * agg.T + bias_outer  1.69 us

commit v1 on v0

v1 whole, which is shorter than its diff:
```python
import functools

import jax
import jax.numpy as jnp
from jax import lax
from jax.experimental import pallas as pl
from jax.experimental.pallas import tpu as pltpu
from jax.sharding import PartitionSpec as P

MESH = pl.DeviceIdType.MESH
NT = (((1,), (1,)), ((), ()))
PARTS = 4
HALVES = 2


class Place:
    def __init__(self, n_dom, n_sub):
        self.n_dom, self.n_sub = n_dom, n_sub
        self.dom, self.sub = lax.axis_index("dom"), lax.axis_index("sub")
        self.mine = self.dom * n_sub + self.sub

    def flip(self, a):
        total, bit = 0, 1
        while bit < self.n_dom:
            total = total + lax.rem(lax.div(self.dom, bit) + lax.div(a, bit), 2) * bit
            bit *= 2
        return total

    def target(self, k):
        n_sub = self.n_sub
        return self.flip(lax.div(k, n_sub)), lax.rem(self.sub + lax.rem(k, n_sub), n_sub)

    def source(self, k):
        n_sub = self.n_sub
        return self.flip(lax.div(k, n_sub)) * n_sub + lax.rem(self.sub + n_sub - lax.rem(k, n_sub), n_sub)


def picked(first, second, table, lists):
    slots = jnp.concatenate([lists[pl.ds(first, 1), :], lists[pl.ds(second, 1), :]], axis=1)
    verts = table.shape[-1]
    hot = lax.broadcasted_iota(jnp.int32, (verts, slots.shape[1]), 0) == slots
    hot = jnp.where(hot, 1.0, 0.0).astype(table.dtype)
    return jnp.dot(table[...], hot, preferred_element_type=jnp.float32).astype(table.dtype)


def add(acc, block, c0, c1, fresh, tiles, where_tile):
    rows, _, blk, _ = tiles.shape

    def tile(r, c):
        t = where_tile[r, c]
        found = tiles[r, jnp.maximum(t, 0)]
        return jnp.where(t >= 0, found, jnp.zeros_like(found))

    for r in range(0, rows, 2):
        weights = jnp.concatenate(
            [jnp.concatenate([tile(r + q, c0), tile(r + q, c1)], axis=1) for q in range(2)], axis=0
        )
        term = lax.dot_general(block, weights, NT, preferred_element_type=jnp.float32)
        span = slice(r * blk, (r + 2) * blk)
        acc[:, span] = term if fresh else acc[:, span] + term


def prologue(place, hbm, staged, tiles_hbm, tiles, tile_sem, stage_sem, found, where_tile, found_sem, proj):
    ft, w_inner, _, _, degrees, _, tile_col = staged
    verts = proj.shape[1]
    part = verts // PARTS
    small = [
        pltpu.make_async_copy(src, dst, stage_sem.at[i])
        for i, (src, dst) in enumerate(zip(hbm, staged))
        if i
    ]
    wide = [
        pltpu.make_async_copy(
            hbm[0].at[:, pl.ds(v * part, part)], ft.at[:, pl.ds(v * part, part)], stage_sem.at[len(staged) + v]
        )
        for v in range(PARTS)
    ]
    small[0].start()
    small[3].start()
    for each in wide:
        each.start()
    for i in (1, 2, 4, 5):
        small[i].start()
    tile_copy = pltpu.make_async_copy(tiles_hbm, tiles, tile_sem)
    tile_copy.start()

    barrier = pltpu.get_barrier_semaphore()
    peers = place.n_dom * place.n_sub

    @pl.loop(1, peers)
    def _(k):
        pl.semaphore_signal(barrier, inc=1, device_id=place.target(k), device_id_type=MESH)

    small[0].wait()
    small[3].wait()
    inv = lax.rsqrt(degrees[...].astype(jnp.float32))
    w_t = w_inner[...].T
    for v in range(PARTS):
        span = slice(v * part, (v + 1) * part)
        wide[v].wait()
        term = jnp.dot(w_t, ft[:, span], preferred_element_type=jnp.float32)
        proj[:, span] = (term * inv[:, span]).astype(proj.dtype)
    for i in (1, 2, 4, 5):
        small[i].wait()
    cols = tile_col[...]
    lane = lax.broadcasted_iota(jnp.int32, found.shape, 1)
    at = jnp.full(found.shape, -1, jnp.int32)
    for t in range(cols.shape[1]):
        at = jnp.where(cols[:, t:t + 1] == lane, t, at)
    found[...] = at
    found_copy = pltpu.make_async_copy(found, where_tile, found_sem)
    found_copy.start()
    pl.semaphore_wait(barrier, peers - 1)
    return inv, tile_copy, found_copy


def score(acc_in, inv, bias_col, w_pad, scores, blk):
    for v in range(0, scores.shape[1], blk):
        span = slice(v, v + blk)
        scale = inv[:, span]
        hidden = scale * jnp.maximum(scale * acc_in[:, span] + bias_col, 0.0)
        scores[:, span] = jnp.dot(
            w_pad[...], hidden.astype(jnp.bfloat16), preferred_element_type=jnp.float32
        ).astype(scores.dtype)


def relay_kernel(n_dom, n_sub, *refs):
    hbm, (tiles_hbm, out), staged, refs = refs[:7], refs[7:9], refs[9:16], refs[16:]
    (
        stage_sem, found, where_tile, found_sem, proj, out_in, got_in, acc_in, w_pad, scores, out_sc, got_sc,
        acc_sc, tiles, tile_sem, send_in, recv_in, send_sc, recv_sc, far_proj, far_lists, proj_send, proj_recv,
        lists_send, lists_recv,
    ) = refs
    _, _, bias, w_outer, _, lists, _ = staged
    place = Place(n_dom, n_sub)
    dom, sub, mine, flip = place.dom, place.sub, place.mine, place.flip
    hid, verts = proj.shape
    blk = tiles.shape[2]
    own = verts // blk
    classes = w_outer.shape[0]
    part = hid // HALVES
    per_step = 2 * n_dom
    half = lax.div(sub, 2)
    sibling, near, far = 1 + 4 * half - sub, 2 - half, 3 - 3 * half
    mid = lax.rem(sub + half, 2)
    middle = mid == 1
    edge = mid == 0

    inv, tile_copy, found_copy = prologue(
        place, hbm, staged, tiles_hbm, tiles, tile_sem, stage_sem, found, where_tile, found_sem, proj
    )

    def lists_copy(slot):
        return pltpu.make_async_remote_copy(
            src_ref=lists, dst_ref=far_lists.at[slot], send_sem=lists_send, recv_sem=lists_recv.at[slot],
            device_id=(dom, near), device_id_type=MESH,
        )

    def piece_copy(slot, c):
        rows = pl.ds(c * part, part)
        return pltpu.make_async_remote_copy(
            src_ref=proj.at[rows], dst_ref=far_proj.at[slot, rows], send_sem=proj_send.at[c],
            recv_sem=proj_recv.at[slot, c], device_id=(dom, near), device_id_type=MESH,
        )

    def send_table(slot):
        lists_copy(slot).start()
        for c in range(HALVES):
            piece_copy(slot, c).start()

    def list_copy(j, e, to_dom, to_sub):
        return pltpu.make_async_remote_copy(
            src_ref=out_in.at[j], dst_ref=got_in.at[e], send_sem=send_in.at[j], recv_sem=recv_in.at[0, e],
            device_id=(to_dom, to_sub), device_id_type=MESH,
        )

    def half_copy(j, e, c, to_dom, to_sub):
        rows = pl.ds(c * part, part)
        return pltpu.make_async_remote_copy(
            src_ref=out_in.at[j, rows], dst_ref=got_in.at[e, rows], send_sem=send_in.at[j],
            recv_sem=recv_in.at[c, e], device_id=(to_dom, to_sub), device_id_type=MESH,
        )

    def hand_out_own():
        def pair(a):
            row = flip(a) * n_sub
            return picked(row + sub, row + sibling, proj, lists)

        first = pair(0)
        got_in[mine] = first[:, :blk]
        out_in[1] = first[:, blk:]
        list_copy(1, mine, dom, sibling).start()

        @pl.loop(1, n_dom)
        def _(a):
            both = pair(a)
            j = 2 * a
            out_in[j] = both[:, :blk]
            out_in[j + 1] = both[:, blk:]
            list_copy(j + 1, mine, flip(a), sibling).start()
            list_copy(j, mine, flip(a), sub).start()

    def relay(slot, c, from_sub):
        if c == 0:
            lists_copy(slot).wait_recv()
        piece_copy(slot, c).wait_recv()
        e = dom * n_sub + from_sub
        base = (slot + 1) * per_step
        rows = slice(c * part, (c + 1) * part)

        def pair(a):
            row = flip(a) * n_sub
            return picked(row + sub, row + sibling, far_proj.at[slot, rows], far_lists.at[slot])

        first = pair(0)
        got_in[e, rows, :] = first[:, :blk]
        out_in[base + 1, rows, :] = first[:, blk:]
        half_copy(base + 1, e, c, dom, sibling).start()

        @pl.loop(1, n_dom)
        def _(a):
            both = pair(a)
            j = base + 2 * a
            out_in[j, rows, :] = both[:, :blk]
            out_in[j + 1, rows, :] = both[:, blk:]
            half_copy(j + 1, e, c, flip(a), sibling).start()
            half_copy(j, e, c, flip(a), sub).start()

    def add_own(table, acc):
        for c in range(0, own, 2):
            add(acc, table[:, c * blk:(c + 2) * blk], c, c + 1, c == 0, tiles, where_tile)

    def pair_of(m, plane):
        return flip(2 * m) * n_sub + plane, flip(2 * m + 1) * n_sub + plane

    def add_whole(m, plane):
        e0, e1 = pair_of(m, plane)
        add(
            acc_in, jnp.concatenate([got_in[e0], got_in[e1]], axis=1), own + e0, own + e1, False, tiles, where_tile
        )

    def add_plane(plane):
        for i, e in enumerate(pair_of(0, plane)):
            if i:
                list_copy(0, e, dom, sibling).wait_recv()
            else:
                @pl.when(plane != sub)
                def _():
                    list_copy(0, e, dom, sibling).wait_recv()
        add_whole(0, plane)

        @pl.loop(1, n_dom // 2)
        def _(m):
            for e in pair_of(m, plane):
                list_copy(0, e, dom, sibling).wait_recv()
            add_whole(m, plane)

    def await_pair(m, plane, c):
        for e in pair_of(m, plane):
            half_copy(0, e, c, dom, sibling).wait_recv()

    def add_relayed(plane):
        _, e1 = pair_of(0, plane)
        for c in range(HALVES):
            half_copy(0, e1, c, dom, sibling).wait_recv()
        add_whole(0, plane)

        @pl.loop(1, n_dom // 2)
        def _(m):
            for c in range(HALVES):
                await_pair(m, plane, c)
            add_whole(m, plane)

    def add_halves(plane, c):
        rows = slice(c * part, (c + 1) * part)

        @pl.loop(0, n_dom // 2)
        def _(m):
            e0, e1 = pair_of(m, plane)
            await_pair(m, plane, c)
            block = jnp.concatenate([got_in[e0, rows, :], got_in[e1, rows, :]], axis=1)
            add(acc_in.at[rows], block, own + e0, own + e1, False, tiles, where_tile)

    pl.when(middle)(lambda: send_table(0))
    hand_out_own()
    pl.when(edge)(lambda: send_table(1))
    w_pad[...] = jnp.zeros_like(w_pad)
    w_pad[0:classes, :] = w_outer[...]
    bias_col = jnp.broadcast_to(bias[...], (blk, hid)).T
    tile_copy.wait()
    found_copy.wait()
    add_own(proj, acc_in)
    add_plane(sub)

    @pl.when(middle)
    def _():
        relay(0, 0, near)
        relay(0, 1, near)
        add_plane(sibling)
        relay(1, 0, far)
        add_relayed(near)
        relay(1, 1, far)
        add_relayed(far)

    @pl.when(edge)
    def _():
        add_plane(sibling)
        for plane in (near, far):
            for c in range(HALVES):
                add_halves(plane, c)

    score(acc_in, inv, bias_col, w_pad, scores, blk)

    def score_copy(k, e, to_dom, to_sub):
        return pltpu.make_async_remote_copy(
            src_ref=out_sc.at[k], dst_ref=got_sc.at[e], send_sem=send_sc.at[k], recv_sem=recv_sc.at[e],
            device_id=(to_dom, to_sub), device_id_type=MESH,
        )

    def deliver(i, plane, last):
        def send(m):
            both = picked(*pair_of(m, plane), scores, lists)
            for q in range(2):
                k = i * n_dom + 2 * m + q
                out_sc[k] = both[:, q * blk:(q + 1) * blk]
                score_copy(k, mine, flip(2 * m + q), plane).start()

        @pl.loop(0, n_dom // 2 - last)
        def _(m):
            send(n_dom // 2 - 1 - m)

        if last:
            both = picked(*pair_of(0, plane), scores, lists)
            got_sc[mine] = both[:, :blk]
            out_sc[i * n_dom + 1] = both[:, blk:]
            score_copy(i * n_dom + 1, mine, flip(1), plane).start()

    def add_scores(m, plane):
        e0, e1 = pair_of(m, plane)
        block = jnp.concatenate([got_sc[e0], got_sc[e1]], axis=1)
        add(acc_sc, block, own + e0, own + e1, False, tiles, where_tile)

    def gather(plane):
        @pl.loop(0, n_dom // 2 - 1)
        def _(i):
            m = n_dom // 2 - 1 - i
            for e in pair_of(m, plane):
                score_copy(0, e, dom, sibling).wait_recv()
            add_scores(m, plane)

        e0, e1 = pair_of(0, plane)

        @pl.when(plane != sub)
        def _():
            score_copy(0, e0, dom, sibling).wait_recv()

        score_copy(0, e1, dom, sibling).wait_recv()
        add_scores(0, plane)

    for i, plane in enumerate((far, near, sibling, sub)):
        deliver(i, plane, int(i == 3))
    add_own(scores, acc_sc)

    @pl.loop(1, per_step)
    def _(j):
        list_copy(j, 0, dom, sibling).wait_send()

    lists_copy(0).wait_send()
    for c in range(HALVES):
        piece_copy(0, c).wait_send()

    @pl.when(middle)
    def _():
        for base in (per_step, 2 * per_step):
            @pl.loop(1, per_step)
            def _(j):
                list_copy(base + j, 0, dom, sibling).wait_send()

    gather(sibling + mid * (sub - sibling))
    gather(near)
    gather(sub + mid * (sibling - sub))

    @pl.loop(0, n_dom * n_sub)
    def _(k):
        @pl.when(k != 3 * n_dom)
        def _():
            score_copy(k, 0, dom, sibling).wait_send()

    gather(far)
    out[...] = inv * acc_sc[0:classes, :]


def direct_kernel(n_dom, n_sub, *refs):
    hbm, (tiles_hbm, out), staged, refs = refs[:7], refs[7:9], refs[9:16], refs[16:]
    (
        stage_sem, found, where_tile, found_sem, proj, out_in, got_in, acc_in, w_pad, scores, out_sc, got_sc,
        acc_sc, tiles, tile_sem, send_in, recv_in, send_sc, recv_sc,
    ) = refs
    _, _, bias, w_outer, _, lists, _ = staged
    place = Place(n_dom, n_sub)
    peers = n_dom * n_sub
    hid, verts = proj.shape
    blk = tiles.shape[2]
    own = verts // blk
    classes = w_outer.shape[0]

    inv, tile_copy, found_copy = prologue(
        place, hbm, staged, tiles_hbm, tiles, tile_sem, stage_sem, found, where_tile, found_sem, proj
    )

    def copy(src, dst, sends, recvs, k):
        return pltpu.make_async_remote_copy(
            src_ref=src.at[k], dst_ref=dst.at[k], send_sem=sends.at[k], recv_sem=recvs.at[k],
            device_id=place.target(k), device_id_type=MESH,
        )

    def pick(k, table):
        index = [to_dom * n_sub + to_sub for to_dom, to_sub in (place.target(k), place.target(k + 1))]
        return picked(*index, table, lists)

    def deliver(table, outgoing, got, sends, recvs):
        first = pick(0, table)
        got[0] = first[:, :blk]
        outgoing[1] = first[:, blk:]
        copy(outgoing, got, sends, recvs, 1).start()

        @pl.loop(1, peers // 2)
        def _(pair):
            k = 2 * pair
            both = pick(k, table)
            outgoing[k] = both[:, :blk]
            outgoing[k + 1] = both[:, blk:]
            copy(outgoing, got, sends, recvs, k).start()
            copy(outgoing, got, sends, recvs, k + 1).start()

    def aggregate(table, outgoing, got, sends, recvs, acc):
        for c in range(0, own, 2):
            add(acc, table[:, c * blk:(c + 2) * blk], c, c + 1, c == 0, tiles, where_tile)

        def arrived(k):
            block = jnp.concatenate([got[k], got[k + 1]], axis=1)
            add(acc, block, own + place.source(k), own + place.source(k + 1), False, tiles, where_tile)

        copy(outgoing, got, sends, recvs, 1).wait_recv()
        arrived(0)

        @pl.loop(1, peers // 2)
        def _(pair):
            k = 2 * pair
            copy(outgoing, got, sends, recvs, k).wait_recv()
            copy(outgoing, got, sends, recvs, k + 1).wait_recv()
            arrived(k)

    deliver(proj, out_in, got_in, send_in, recv_in)
    w_pad[...] = jnp.zeros_like(w_pad)
    w_pad[0:classes, :] = w_outer[...]
    bias_col = jnp.broadcast_to(bias[...], (blk, hid)).T
    tile_copy.wait()
    found_copy.wait()
    aggregate(proj, out_in, got_in, send_in, recv_in, acc_in)
    score(acc_in, inv, bias_col, w_pad, scores, blk)
    deliver(scores, out_sc, got_sc, send_sc, recv_sc)
    aggregate(scores, out_sc, got_sc, send_sc, recv_sc, acc_sc)
    out[...] = inv * acc_sc[0:classes, :]

    @pl.loop(1, peers)
    def _(k):
        copy(out_in, got_in, send_in, recv_in, k).wait_send()
        copy(out_sc, got_sc, send_sc, recv_sc, k).wait_send()


def on_device(
    n_dom, n_sub,
    features, w_inner, bias_inner, w_outer, bias_outer, tiles, tile_col, degrees, send_rows
):
    peers = n_dom * n_sub
    verts, hid = features.shape[0], w_inner.shape[1]
    classes = w_outer.shape[1]
    padded = 16 * ((classes + 15) // 16)
    blk = tiles.shape[2]
    columns = verts // blk + peers
    lanes = 128 * ((columns + 127) // 128)
    small = (
        features.T, w_inner, bias_inner[None, :], w_outer.T, degrees[None, :], send_rows[0], tile_col
    )
    relay = n_sub == 4
    lists_out = 6 * n_dom if relay else peers
    vmem = pl.BlockSpec(memory_space=pltpu.VMEM)
    bf16, f32 = jnp.bfloat16, jnp.float32
    agg = pl.pallas_call(
        functools.partial(relay_kernel if relay else direct_kernel, n_dom, n_sub),
        out_shape=jax.ShapeDtypeStruct((classes, verts), f32),
        in_specs=[pl.BlockSpec(memory_space=pl.ANY)] * 8,
        out_specs=vmem,
        scratch_shapes=[pltpu.VMEM(each.shape, each.dtype) for each in small]
        + [
            pltpu.SemaphoreType.DMA((len(small) + PARTS,)),
            pltpu.VMEM((tiles.shape[0], lanes), jnp.int32),
            pltpu.SMEM((tiles.shape[0], lanes), jnp.int32),
            pltpu.SemaphoreType.DMA,
            pltpu.VMEM((hid, verts), bf16),
            pltpu.VMEM((lists_out, hid, blk), bf16),
            pltpu.VMEM((peers, hid, blk), bf16),
            pltpu.VMEM((hid, verts), f32),
            pltpu.VMEM((padded, hid), bf16),
            pltpu.VMEM((padded, verts), bf16),
            pltpu.VMEM((peers, padded, blk), bf16),
            pltpu.VMEM((peers, padded, blk), bf16),
            pltpu.VMEM((padded, verts), f32),
            pltpu.VMEM(tiles.shape, bf16),
            pltpu.SemaphoreType.DMA,
            pltpu.SemaphoreType.DMA((lists_out,)),
            pltpu.SemaphoreType.DMA((HALVES, peers) if relay else (peers,)),
            pltpu.SemaphoreType.DMA((peers,)),
            pltpu.SemaphoreType.DMA((peers,)),
        ]
        + (
            [
                pltpu.VMEM((2, hid, verts), bf16),
                pltpu.VMEM((2, peers, blk), jnp.int32),
                pltpu.SemaphoreType.DMA((HALVES,)),
                pltpu.SemaphoreType.DMA((2, HALVES)),
                pltpu.SemaphoreType.DMA,
                pltpu.SemaphoreType.DMA((2,)),
            ]
            if relay
            else []
        ),
        compiler_params=pltpu.CompilerParams(
            collective_id=0, has_side_effects=True, vmem_limit_bytes=56 * 1024 * 1024
        ),
    )(*small, tiles)
    return agg.T + bias_outer


def solution(mesh):
    return jax.shard_map(
        functools.partial(on_device, mesh.shape["dom"], mesh.shape["sub"]),
        mesh=mesh,
        in_specs=(
            P(("dom", "sub"), None),
            P(),
            P(),
            P(),
            P(),
            P(("dom", "sub"), None, None, None),
            P(("dom", "sub"), None),
            P(("dom", "sub")),
            P(("dom", "sub"), None, None),
        ),
        out_specs=P(("dom", "sub"), None),
        check_vma=False,
    )
```

time: 66.1 us -> 65.1 us (0.985)
  other arithmetic: 2.39 us -> 1.69 us
    rsqrt x1 -> x0, other arithmetic: 0.7 us -> none  [on_device(): inv_sqrt = lax.rsqrt(degrees.astype(f32))[:, None]]
where the time goes in v1:
time: 65.1 us; the launch traced here: 65 us
  Pallas kernels  63.3 us (97%)
  other arithmetic  1.69 us (3%)
    pallas_call x1, Pallas kernels, on_device(): pl.pallas_call(functools.partial(relay_kernel if relay else direct_kernel...  63.3 us
    add x1, other arithmetic, on_device(): return agg.T + bias_outer  1.69 us

profile of v1, /device:TPU:0, one launch (start us, length us, event | category | flops | bytes accessed | tf_op | source)
XLA Modules:
  0.0 65.0 jit_solution(17417323518458493470)
XLA Ops:
  0.0 0.0 copy-start
  0.0 63.3 %shard_map.91 = f32[41,1024]{1,0:T(8,128)} custom-call(bf16[602,1024]{1,0:T(8,128)(2,1)} %bitcast.7, bf16[602,256]{1,0:T(8,128)(2,1)} %refs_1_.1, f32[1,256]{1,0:T(1,128)} %bitcast.11, bf16[41,256]{1,0:T(8,128)(2,1)} %bitcast.8, s32[1,1024]{1,0:T(1,128)} %bitcast.10, s32[32,128]{1,0:T(8,128)} %bitcast.9, s32[8,32]{1,0:T(8,128)} %refs_6_.1, ...), custom_call_target="tpu_custom_call" | custom-call | tf_op jit(solution)/shard_map/pallas_call | solution.py:490
  63.3 0.0 copy-done
  63.3 1.7 %add_bitcast_fusion = f32[1024,41]{0,1:T(8,128)} fusion(f32[41,1024]{1,0:T(8,128)} %shard_map.91, f32[41]{0:T(128)S(1)} %copy-done), kind=kLoop, calls=%fused_computation | loop fusion | flops 41984 | bytes 336036 | tf_op jit(solution)/shard_map/add | solution.py:533
Async XLA Ops:
  0.0 63.3 %copy-start = (f32[41]{0:T(128)S(1)}, f32[41]{0:T(128)}, u32[]{:S(2)}) copy-start(f32[41]{0:T(128)} %param.13) | copy-start | bytes 496

commit v2 on v1

v2 whole, which is shorter than its diff:
```python
import functools

import jax
import jax.numpy as jnp
from jax import lax
from jax.experimental import pallas as pl
from jax.experimental.pallas import tpu as pltpu
from jax.sharding import PartitionSpec as P

MESH = pl.DeviceIdType.MESH
NT = (((1,), (1,)), ((), ()))
PARTS = 4
HALVES = 2


class Place:
    def __init__(self, n_dom, n_sub):
        self.n_dom, self.n_sub = n_dom, n_sub
        self.dom, self.sub = lax.axis_index("dom"), lax.axis_index("sub")
        self.mine = self.dom * n_sub + self.sub

    def flip(self, a):
        total, bit = 0, 1
        while bit < self.n_dom:
            total = total + lax.rem(lax.div(self.dom, bit) + lax.div(a, bit), 2) * bit
            bit *= 2
        return total

    def target(self, k):
        n_sub = self.n_sub
        return self.flip(lax.div(k, n_sub)), lax.rem(self.sub + lax.rem(k, n_sub), n_sub)

    def source(self, k):
        n_sub = self.n_sub
        return self.flip(lax.div(k, n_sub)) * n_sub + lax.rem(self.sub + n_sub - lax.rem(k, n_sub), n_sub)


def hot_of(first, second, lists, verts):
    slots = jnp.concatenate([lists[pl.ds(first, 1), :], lists[pl.ds(second, 1), :]], axis=1)
    hot = lax.broadcasted_iota(jnp.int32, (verts, slots.shape[1]), 0) == slots
    return jnp.where(hot, 1.0, 0.0).astype(jnp.bfloat16)


def taken(table, hot):
    return jnp.dot(table[...], hot, preferred_element_type=jnp.float32).astype(table.dtype)


def picked(first, second, table, lists):
    return taken(table, hot_of(first, second, lists, table.shape[-1]))


def add(acc, block, c0, c1, fresh, tiles, where_tile):
    rows, _, blk, _ = tiles.shape

    def tile(r, c):
        t = where_tile[r, c]
        found = tiles[r, jnp.maximum(t, 0)]
        return jnp.where(t >= 0, found, jnp.zeros_like(found))

    for r in range(0, rows, 2):
        weights = jnp.concatenate(
            [jnp.concatenate([tile(r + q, c0), tile(r + q, c1)], axis=1) for q in range(2)], axis=0
        )
        term = lax.dot_general(block, weights, NT, preferred_element_type=jnp.float32)
        span = slice(r * blk, (r + 2) * blk)
        acc[:, span] = term if fresh else acc[:, span] + term


def prologue(place, hbm, staged, tiles_hbm, tiles, tile_sem, stage_sem, found, where_tile, found_sem, proj, greet):
    ft, w_inner, _, _, degrees, _, tile_col = staged
    verts = proj.shape[1]
    part = verts // PARTS
    small = [
        pltpu.make_async_copy(src, dst, stage_sem.at[i])
        for i, (src, dst) in enumerate(zip(hbm, staged))
        if i
    ]
    wide = [
        pltpu.make_async_copy(
            hbm[0].at[:, pl.ds(v * part, part)], ft.at[:, pl.ds(v * part, part)], stage_sem.at[len(staged) + v]
        )
        for v in range(PARTS)
    ]
    small[0].start()
    small[3].start()
    for each in wide:
        each.start()
    for i in (1, 2, 4, 5):
        small[i].start()
    tile_copy = pltpu.make_async_copy(tiles_hbm, tiles, tile_sem)

    greet()

    small[0].wait()
    small[3].wait()
    inv = lax.rsqrt(degrees[...].astype(jnp.float32))
    w_t = w_inner[...].T
    for v in range(PARTS):
        span = slice(v * part, (v + 1) * part)
        wide[v].wait()
        term = jnp.dot(w_t, ft[:, span], preferred_element_type=jnp.float32)
        if v == PARTS - 1:
            tile_copy.start()
        proj[:, span] = (term * inv[:, span]).astype(proj.dtype)
    for i in (1, 2, 4, 5):
        small[i].wait()
    cols = tile_col[...]
    lane = lax.broadcasted_iota(jnp.int32, found.shape, 1)
    at = jnp.full(found.shape, -1, jnp.int32)
    for t in range(cols.shape[1]):
        at = jnp.where(cols[:, t:t + 1] == lane, t, at)
    found[...] = at
    found_copy = pltpu.make_async_copy(found, where_tile, found_sem)
    found_copy.start()
    return inv, tile_copy, found_copy


def turn_of(i, count):
    return count - 1 - lax.div(i, 2) - count // 2 * lax.rem(i, 2)


def score(acc_in, inv, bias_col, w_pad, scores, blk):
    for v in range(0, scores.shape[1], blk):
        span = slice(v, v + blk)
        scale = inv[:, span]
        hidden = scale * jnp.maximum(scale * acc_in[:, span] + bias_col, 0.0)
        scores[:, span] = jnp.dot(
            w_pad[...], hidden.astype(jnp.bfloat16), preferred_element_type=jnp.float32
        ).astype(scores.dtype)


def relay_kernel(n_dom, n_sub, *refs):
    hbm, (tiles_hbm, out), staged, refs = refs[:7], refs[7:9], refs[9:16], refs[16:]
    (
        stage_sem, found, where_tile, found_sem, proj, out_in, got_in, acc_in, w_pad, scores, out_sc, got_sc,
        acc_sc, tiles, tile_sem, send_in, recv_in, send_sc, recv_sc, far_proj, far_lists, proj_send, proj_recv,
        lists_send, lists_recv, dense, hots, clear,
    ) = refs
    _, _, bias, w_outer, _, lists, _ = staged
    place = Place(n_dom, n_sub)
    dom, sub, flip = place.dom, place.sub, place.flip
    hid, verts = proj.shape
    blk = tiles.shape[2]
    own = verts // blk
    classes = w_outer.shape[0]
    part = hid // HALVES
    pairs = n_dom // 2
    per_step = 2 * n_dom
    peers = n_dom * n_sub
    half = lax.div(sub, 2)
    sibling, near, far = 1 + 4 * half - sub, 2 - half, 3 - 3 * half
    mid = lax.rem(sub + half, 2)
    middle, edge = mid == 1, mid == 0
    barrier = pltpu.get_barrier_semaphore()

    def greet():
        @pl.loop(1, peers)
        def _(k):
            pl.semaphore_signal(barrier, inc=1, device_id=place.target(k), device_id_type=MESH)

    inv, tile_copy, found_copy = prologue(
        place, hbm, staged, tiles_hbm, tiles, tile_sem, stage_sem, found, where_tile, found_sem, proj, greet
    )

    def lists_copy(slot):
        return pltpu.make_async_remote_copy(
            src_ref=lists, dst_ref=far_lists.at[slot], send_sem=lists_send, recv_sem=lists_recv.at[slot],
            device_id=(dom, near), device_id_type=MESH,
        )

    def piece_copy(slot, c):
        rows = pl.ds(c * part, part)
        return pltpu.make_async_remote_copy(
            src_ref=proj.at[rows], dst_ref=far_proj.at[slot, rows], send_sem=proj_send,
            recv_sem=proj_recv.at[slot, c], device_id=(dom, near), device_id_type=MESH,
        )

    def send_table(slot):
        lists_copy(slot).start()
        for c in range(HALVES):
            piece_copy(slot, c).start()

    def await_table():
        lists_copy(0).wait_send()
        pltpu.make_async_remote_copy(
            src_ref=proj, dst_ref=far_proj.at[0], send_sem=proj_send, recv_sem=proj_recv.at[0, 0],
            device_id=(dom, near), device_id_type=MESH,
        ).wait_send()

    def came_in(plane, m, c):
        return recv_in.at[(n_sub * pairs + lax.rem(plane, 2) * pairs if c else plane * pairs) + m]

    def lists_of(ref, at, c):
        return ref.at[at] if c is None else ref.at[at, pl.ds(c * part, part)]

    def list_copy(j, plane, a, c, to_sub, relayed):
        return pltpu.make_async_remote_copy(
            src_ref=lists_of(out_in, j, c), dst_ref=lists_of(got_in, plane * n_dom + a, c),
            send_sem=send_in.at[relayed], recv_sem=came_in(plane, lax.div(a, 2), c),
            device_id=(flip(a), to_sub), device_id_type=MESH,
        )

    def await_lists(plane, m, c, count=2):
        at = pl.ds(plane * n_dom + 2 * m + 2 - count, count)
        pltpu.make_async_remote_copy(
            src_ref=lists_of(out_in, pl.ds(0, count), c), dst_ref=lists_of(got_in, at, c),
            send_sem=send_in.at[0], recv_sem=came_in(plane, m, c),
            device_id=(dom, sibling), device_id_type=MESH,
        ).wait_recv()

    def await_sent(relayed, count):
        pltpu.make_async_remote_copy(
            src_ref=out_in.at[pl.ds(0, count)], dst_ref=out_in.at[pl.ds(0, count)],
            send_sem=send_in.at[relayed], recv_sem=recv_in.at[0],
            device_id=(dom, sibling), device_id_type=MESH,
        ).wait_send()

    def keep_hot(a, hot, first, second):
        at = pl.ds(pl.multiple_of(a * blk, blk), blk)
        hots[first, :, at] = hot[:, :blk]
        hots[second, :, at] = hot[:, blk:]

    def pick_own(a):
        row = flip(a) * n_sub
        hot = hot_of(row + sub, row + sibling, lists, verts)
        keep_hot(a, hot, sub, sibling)
        both = taken(proj, hot)
        out_in[2 * a + 1] = both[:, blk:]
        return both[:, :blk]

    def pick_both(a):
        out_in[2 * a] = pick_own(a)

    def send_both(a):
        list_copy(2 * a + 1, sub, a, None, sibling, 0).start()
        list_copy(2 * a, sub, a, None, sub, 0).start()

    def hand_out_own():
        send_both(n_dom - 1)

        @pl.loop(1, n_dom - 1)
        def _(i):
            pick_both(turn_of(i, n_dom))
            send_both(turn_of(i, n_dom))

        got_in[sub * n_dom] = pick_own(0)
        list_copy(1, sub, 0, None, sibling, 0).start()

    def turn(begin, end, column_of, at):
        def tile(r, c):
            t = where_tile[r, c]
            found = tiles[r, jnp.maximum(t, 0)]
            return jnp.where(t >= 0, found, jnp.zeros_like(found))

        @pl.loop(begin, end)
        def _(i):
            c = column_of(i)
            for r in range(0, tiles.shape[0], 2):
                both = jnp.concatenate([tile(r, c), tile(r + 1, c)], axis=0)
                dense[at + i, :, r * blk:(r + 2) * blk] = both.T

    def turn_slots(begin, end):
        turn(begin, end, lambda i: own + flip(lax.rem(i, n_dom)) * n_sub + lax.div(i, n_dom), own)

    def keep_far_hots():
        @pl.loop(0, n_dom)
        def _(a):
            row = flip(a) * n_sub
            keep_hot(a, hot_of(row + near, row + far, lists, verts), near, far)

    def relay(slot, c, plane):
        if c == 0:
            lists_copy(slot).wait_recv()
        piece_copy(slot, c).wait_recv()
        base = (slot + 1) * per_step
        rows = slice(c * part, (c + 1) * part)

        def pair(a):
            row = flip(a) * n_sub
            return picked(row + sub, row + sibling, far_proj.at[slot, rows], far_lists.at[slot])

        @pl.loop(0, n_dom - 1)
        def _(i):
            a = turn_of(i, n_dom)
            both = pair(a)
            j = base + 2 * a
            out_in[j, rows, :] = both[:, :blk]
            out_in[j + 1, rows, :] = both[:, blk:]
            list_copy(j + 1, plane, a, c, sibling, 1).start()
            list_copy(j, plane, a, c, sub, 1).start()

        first = pair(0)
        got_in[plane * n_dom, rows, :] = first[:, :blk]
        out_in[base + 1, rows, :] = first[:, blk:]
        list_copy(base + 1, plane, 0, c, sibling, 1).start()

    wide = 2 * blk

    def add_dense(acc, block, first, count, fresh):
        for v in range(0, verts, wide):
            span = slice(v, v + wide)
            weights = dense[pl.ds(first, count), :, span].reshape(count * blk, wide)
            term = jnp.dot(block, weights, preferred_element_type=jnp.float32)
            acc[:, span] = term if fresh else acc[:, span] + term

    def add_own(table, acc):
        add_dense(acc, table[...], 0, own, True)

    def add_pair(plane, m):
        slot = plane * n_dom + 2 * m
        add_dense(acc_in, jnp.concatenate([got_in[slot], got_in[slot + 1]], axis=1), own + slot, 2, False)

    def add_plane(plane, halves, local):
        parts = range(HALVES) if halves else (None,)

        @pl.loop(0, pairs - 1)
        def _(i):
            m = turn_of(i, pairs)
            for c in parts:
                await_lists(plane, m, c)
            add_pair(plane, m)

        for c in parts:
            await_lists(plane, 0, c, 1 if local else 2)
        add_pair(plane, 0)

    def add_halves(plane, c):
        rows = slice(c * part, (c + 1) * part)

        @pl.loop(0, pairs)
        def _(i):
            m = turn_of(i, pairs)
            slot = plane * n_dom + 2 * m
            await_lists(plane, m, c)
            block = jnp.concatenate([got_in[slot, rows, :], got_in[slot + 1, rows, :]], axis=1)
            add_dense(acc_in.at[rows], block, own + slot, 2, False)

    pick_both(n_dom - 1)
    pl.semaphore_wait(barrier, peers - 1)
    pl.when(middle)(lambda: send_table(0))
    hand_out_own()
    w_pad[...] = jnp.zeros_like(w_pad)
    w_pad[0:classes, :] = w_outer[...]
    bias_col = jnp.broadcast_to(bias[...], (blk, hid)).T
    tile_copy.wait()
    found_copy.wait()
    turn(0, own, lambda i: i, 0)
    turn_slots(0, n_dom)
    keep_far_hots()

    @pl.when(middle)
    def _():
        relay(0, 0, near)
        turn_slots(n_dom, 2 * n_dom)
        await_table()
        pl.semaphore_signal(clear, inc=1, device_id=(dom, sibling), device_id_type=MESH)
        turn_slots(2 * n_dom, peers)
        relay(0, 1, near)
        add_own(proj, acc_in)
        add_plane(sub, False, True)
        relay(1, 0, far)
        add_plane(sibling, False, False)
        relay(1, 1, far)
        add_plane(near, True, True)
        add_plane(far, True, True)

    @pl.when(edge)
    def _():
        turn_slots(n_dom, peers)
        add_own(proj, acc_in)
        pl.semaphore_wait(clear, 1)
        send_table(1)
        add_plane(sub, False, True)
        add_plane(sibling, False, False)
        add_halves(near, 0)
        add_halves(near, 1)
        add_halves(far, 0)
        add_halves(far, 1)

    score(acc_in, inv, bias_col, w_pad, scores, blk)

    def score_copy(k, a, plane):
        return pltpu.make_async_remote_copy(
            src_ref=out_sc.at[k], dst_ref=got_sc.at[sub * n_dom + a], send_sem=send_sc, recv_sem=recv_sc.at[sub],
            device_id=(flip(a), plane), device_id_type=MESH,
        )

    def deliver(plane):
        lists_for = taken(scores, hots[plane])
        for a in [n_dom - 1 - i // 2 - n_dom // 2 * (i % 2) for i in range(n_dom)]:
            k = plane * n_dom + a
            out_sc[k] = lists_for[:, a * blk:(a + 1) * blk]
            if a:
                score_copy(k, a, plane).start()
            else:
                pl.when(sub != plane)(lambda: score_copy(k, 0, plane).start())

        @pl.when(sub == plane)
        def _():
            got_sc[sub * n_dom] = lists_for[:, :blk]

    def scores_wait(at, count, plane):
        return pltpu.make_async_remote_copy(
            src_ref=out_sc.at[pl.ds(0, count)], dst_ref=got_sc.at[pl.ds(at, count)], send_sem=send_sc,
            recv_sem=recv_sc.at[plane], device_id=(dom, sibling), device_id_type=MESH,
        )

    def gather(plane):
        slot = plane * n_dom
        pl.when(plane != sub)(lambda: scores_wait(slot, n_dom, plane).wait_recv())
        pl.when(plane == sub)(lambda: scores_wait(slot + 1, n_dom - 1, plane).wait_recv())
        block = jnp.concatenate([got_sc[slot + a] for a in range(n_dom)], axis=1)
        add_dense(acc_sc, block, own + slot, n_dom, False)

    @pl.when(middle)
    def _():
        for plane in (sub, near, sibling):
            deliver(plane)
        await_sent(1, 2 * (per_step - 1))
        deliver(far)

    @pl.when(edge)
    def _():
        for plane in (far, sub, near, sibling):
            deliver(plane)

    add_own(scores, acc_sc)
    await_sent(0, per_step - 1)
    pl.when(edge)(await_table)
    gather(sibling + mid * (sub - sibling))
    gather(near)
    gather(sub + mid * (sibling - sub))
    gather(far)
    out[...] = inv * acc_sc[0:classes, :]
    scores_wait(0, peers - 1, 0).wait_send()


def direct_kernel(n_dom, n_sub, *refs):
    hbm, (tiles_hbm, out), staged, refs = refs[:7], refs[7:9], refs[9:16], refs[16:]
    (
        stage_sem, found, where_tile, found_sem, proj, out_in, got_in, acc_in, w_pad, scores, out_sc, got_sc,
        acc_sc, tiles, tile_sem, send_in, recv_in, send_sc, recv_sc,
    ) = refs
    _, _, bias, w_outer, _, lists, _ = staged
    place = Place(n_dom, n_sub)
    peers = n_dom * n_sub
    hid, verts = proj.shape
    blk = tiles.shape[2]
    own = verts // blk
    classes = w_outer.shape[0]

    barrier = pltpu.get_barrier_semaphore()

    def greet():
        @pl.loop(1, peers)
        def _(k):
            pl.semaphore_signal(barrier, inc=1, device_id=place.target(k), device_id_type=MESH)

    inv, tile_copy, found_copy = prologue(
        place, hbm, staged, tiles_hbm, tiles, tile_sem, stage_sem, found, where_tile, found_sem, proj, greet
    )
    pl.semaphore_wait(barrier, peers - 1)

    def copy(src, dst, sends, recvs, k):
        return pltpu.make_async_remote_copy(
            src_ref=src.at[k], dst_ref=dst.at[k], send_sem=sends.at[k], recv_sem=recvs.at[k],
            device_id=place.target(k), device_id_type=MESH,
        )

    def pick(k, table):
        index = [to_dom * n_sub + to_sub for to_dom, to_sub in (place.target(k), place.target(k + 1))]
        return picked(*index, table, lists)

    def deliver(table, outgoing, got, sends, recvs):
        first = pick(0, table)
        got[0] = first[:, :blk]
        outgoing[1] = first[:, blk:]
        copy(outgoing, got, sends, recvs, 1).start()

        @pl.loop(1, peers // 2)
        def _(pair):
            k = 2 * pair
            both = pick(k, table)
            outgoing[k] = both[:, :blk]
            outgoing[k + 1] = both[:, blk:]
            copy(outgoing, got, sends, recvs, k).start()
            copy(outgoing, got, sends, recvs, k + 1).start()

    def aggregate(table, outgoing, got, sends, recvs, acc):
        for c in range(0, own, 2):
            add(acc, table[:, c * blk:(c + 2) * blk], c, c + 1, c == 0, tiles, where_tile)

        def arrived(k):
            block = jnp.concatenate([got[k], got[k + 1]], axis=1)
            add(acc, block, own + place.source(k), own + place.source(k + 1), False, tiles, where_tile)

        copy(outgoing, got, sends, recvs, 1).wait_recv()
        arrived(0)

        @pl.loop(1, peers // 2)
        def _(pair):
            k = 2 * pair
            copy(outgoing, got, sends, recvs, k).wait_recv()
            copy(outgoing, got, sends, recvs, k + 1).wait_recv()
            arrived(k)

    deliver(proj, out_in, got_in, send_in, recv_in)
    w_pad[...] = jnp.zeros_like(w_pad)
    w_pad[0:classes, :] = w_outer[...]
    bias_col = jnp.broadcast_to(bias[...], (blk, hid)).T
    tile_copy.wait()
    found_copy.wait()
    aggregate(proj, out_in, got_in, send_in, recv_in, acc_in)
    score(acc_in, inv, bias_col, w_pad, scores, blk)
    deliver(scores, out_sc, got_sc, send_sc, recv_sc)
    aggregate(scores, out_sc, got_sc, send_sc, recv_sc, acc_sc)
    out[...] = inv * acc_sc[0:classes, :]

    @pl.loop(1, peers)
    def _(k):
        copy(out_in, got_in, send_in, recv_in, k).wait_send()
        copy(out_sc, got_sc, send_sc, recv_sc, k).wait_send()


def on_device(
    n_dom, n_sub,
    features, w_inner, bias_inner, w_outer, bias_outer, tiles, tile_col, degrees, send_rows
):
    peers = n_dom * n_sub
    verts, hid = features.shape[0], w_inner.shape[1]
    classes = w_outer.shape[1]
    padded = 16 * ((classes + 15) // 16)
    blk = tiles.shape[2]
    columns = verts // blk + peers
    lanes = 128 * ((columns + 127) // 128)
    small = (
        features.T, w_inner, bias_inner[None, :], w_outer.T, degrees[None, :], send_rows[0], tile_col
    )
    relay = n_sub == 4
    lists_out = 6 * n_dom if relay else peers
    vmem = pl.BlockSpec(memory_space=pltpu.VMEM)
    bf16, f32 = jnp.bfloat16, jnp.float32
    agg = pl.pallas_call(
        functools.partial(relay_kernel if relay else direct_kernel, n_dom, n_sub),
        out_shape=pltpu.VMEM((classes, verts), f32),
        in_specs=[pl.BlockSpec(memory_space=pl.ANY)] * 8,
        out_specs=vmem,
        scratch_shapes=[pltpu.VMEM(each.shape, each.dtype) for each in small]
        + [
            pltpu.SemaphoreType.DMA((len(small) + PARTS,)),
            pltpu.VMEM((tiles.shape[0], lanes), jnp.int32),
            pltpu.SMEM((tiles.shape[0], lanes), jnp.int32),
            pltpu.SemaphoreType.DMA,
            pltpu.VMEM((hid, verts), bf16),
            pltpu.VMEM((lists_out, hid, blk), bf16),
            pltpu.VMEM((peers, hid, blk), bf16),
            pltpu.VMEM((hid, verts), f32),
            pltpu.VMEM((padded, hid), bf16),
            pltpu.VMEM((padded, verts), bf16),
            pltpu.VMEM((peers, padded, blk), bf16),
            pltpu.VMEM((peers, padded, blk), bf16),
            pltpu.VMEM((padded, verts), f32),
            pltpu.VMEM(tiles.shape, bf16),
            pltpu.SemaphoreType.DMA,
            pltpu.SemaphoreType.DMA((2 if relay else peers,)),
            pltpu.SemaphoreType.DMA(((n_sub + 2) * n_dom // 2 if relay else peers,)),
            pltpu.SemaphoreType.DMA if relay else pltpu.SemaphoreType.DMA((peers,)),
            pltpu.SemaphoreType.DMA((n_sub if relay else peers,)),
        ]
        + (
            [
                pltpu.VMEM((2, hid, verts), bf16),
                pltpu.VMEM((2, peers, blk), jnp.int32),
                pltpu.SemaphoreType.DMA,
                pltpu.SemaphoreType.DMA((2, HALVES)),
                pltpu.SemaphoreType.DMA,
                pltpu.SemaphoreType.DMA((2,)),
                pltpu.VMEM((columns, blk, verts), bf16),
                pltpu.VMEM((n_sub, verts, n_dom * blk), bf16),
                pltpu.SemaphoreType.REGULAR,
            ]
            if relay
            else []
        ),
        compiler_params=pltpu.CompilerParams(
            collective_id=0, has_side_effects=True, vmem_limit_bytes=56 * 1024 * 1024
        ),
    )(*small, tiles)
    return agg.T + bias_outer


def solution(mesh):
    return jax.shard_map(
        functools.partial(on_device, mesh.shape["dom"], mesh.shape["sub"]),
        mesh=mesh,
        in_specs=(
            P(("dom", "sub"), None),
            P(),
            P(),
            P(),
            P(),
            P(("dom", "sub"), None, None, None),
            P(("dom", "sub"), None),
            P(("dom", "sub")),
            P(("dom", "sub"), None, None),
        ),
        out_specs=P(("dom", "sub"), None),
        check_vma=False,
    )
```

time: 65.1 us -> 52.2 us (0.80)
  Pallas kernels: 63.3 us -> 51.2 us
  other arithmetic: 1.69 us -> 0.76 us
    pallas_call x1, Pallas kernels: 63.3 us -> 51.2 us  [on_device(): pl.pallas_call(functools.partial(relay_kernel if relay else direct_kernel...]
    add x1, other arithmetic: 1.69 us -> 0.76 us  [on_device(): return agg.T + bias_outer]
where the time goes in v2:
time: 52.2 us; the launch traced here: 52 us
  Pallas kernels  51.2 us (98%)
  other arithmetic  0.76 us (1%)
    pallas_call x1, Pallas kernels, on_device(): pl.pallas_call(functools.partial(relay_kernel if relay else direct_kernel...  51.2 us

profile of v2, /device:TPU:0, one launch (start us, length us, event | category | flops | bytes accessed | tf_op | source)
XLA Modules:
  0.0 52.0 jit_solution(1487375389819044513)
XLA Ops:
  0.0 0.0 copy-start
  0.0 51.2 %shard_map.91 = f32[41,1024]{1,0:T(8,128)S(1)} custom-call(bf16[602,1024]{1,0:T(8,128)(2,1)} %bitcast.7, bf16[602,256]{1,0:T(8,128)(2,1)} %refs_1_.1, f32[1,256]{1,0:T(1,128)} %bitcast.11, bf16[41,256]{1,0:T(8,128)(2,1)} %bitcast.8, s32[1,1024]{1,0:T(1,128)} %bitcast.10, s32[32,128]{1,0:T(8,128)} %bitcast.9, s32[8,32]{1,0:T(8,128)} %refs_6_.1, ...), custom_call_target="tpu_custom_call" | custom-call | tf_op jit(solution)/shard_map/pallas_call | solution.py:543
  51.2 0.0 copy-done
  51.2 0.8 %add_bitcast_fusion = f32[1024,41]{0,1:T(8,128)} fusion(f32[41,1024]{1,0:T(8,128)S(1)} %shard_map.91, f32[41]{0:T(128)S(1)} %copy-done), kind=kLoop, calls=%fused_computation | loop fusion | flops 41984 | bytes 336036 | tf_op jit(solution)/shard_map/add | solution.py:589
Async XLA Ops:
  0.0 51.2 %copy-start = (f32[41]{0:T(128)S(1)}, f32[41]{0:T(128)}, u32[]{:S(2)}) copy-start(f32[41]{0:T(128)} %param.13) | copy-start | bytes 496

commit v3 on v2

--- a/solution.py
+++ b/solution.py
@@ -9,7 +9,7 @@
 
 MESH = pl.DeviceIdType.MESH
 NT = (((1,), (1,)), ((), ()))
-PARTS = 4
+PARTS = 2
 HALVES = 2
 
 
@@ -119,6 +119,11 @@
     return count - 1 - lax.div(i, 2) - count // 2 * lax.rem(i, 2)
 
 
+def partner_of(i, count):
+    a = turn_of(i, count)
+    return a + 1 - 2 * lax.rem(a, 2)
+
+
 def score(acc_in, inv, bias_col, w_pad, scores, blk):
     for v in range(0, scores.shape[1], blk):
         span = slice(v, v + blk)
@@ -135,6 +140,7 @@
         stage_sem, found, where_tile, found_sem, proj, out_in, got_in, acc_in, w_pad, scores, out_sc, got_sc,
         acc_sc, tiles, tile_sem, send_in, recv_in, send_sc, recv_sc, far_proj, far_lists, proj_send, proj_recv,
         lists_send, lists_recv, dense, hots, clear,
+        passed_hots, far_scores, table_send, table_recv,
     ) = refs
     _, _, bias, w_outer, _, lists, _ = staged
     place = Place(n_dom, n_sub)
@@ -154,9 +160,11 @@
     barrier = pltpu.get_barrier_semaphore()
 
     def greet():
-        @pl.loop(1, peers)
-        def _(k):
-            pl.semaphore_signal(barrier, inc=1, device_id=place.target(k), device_id_type=MESH)
+        doms = [lax.rem(dom + d, n_dom) for d in range(n_dom)]
+        for step in range(1, n_sub + 1):
+            to_sub = lax.rem(sub + step, n_sub)
+            for to_dom in doms[step // n_sub:]:
+                pl.semaphore_signal(barrier, inc=1, device_id=(to_dom, to_sub), device_id_type=MESH)
 
     inv, tile_copy, found_copy = prologue(
         place, hbm, staged, tiles_hbm, tiles, tile_sem, stage_sem, found, where_tile, found_sem, proj, greet
@@ -229,22 +237,25 @@
         return both[:, :blk]
 
     def pick_both(a):
-        out_in[2 * a] = pick_own(a)
+        mine = pick_own(a)
+        out_in[2 * a] = mine
+
+        @pl.when(a == 0)
+        def _():
+            got_in[sub * n_dom] = mine
 
     def send_both(a):
         list_copy(2 * a + 1, sub, a, None, sibling, 0).start()
-        list_copy(2 * a, sub, a, None, sub, 0).start()
+        pl.when(a != 0)(lambda: list_copy(2 * a, sub, a, None, sub, 0).start())
 
     def hand_out_own():
-        send_both(n_dom - 1)
-
-        @pl.loop(1, n_dom - 1)
+        send_both(partner_of(0, n_dom))
+
+        @pl.loop(1, n_dom)
         def _(i):
-            pick_both(turn_of(i, n_dom))
-            send_both(turn_of(i, n_dom))
-
-        got_in[sub * n_dom] = pick_own(0)
-        list_copy(1, sub, 0, None, sibling, 0).start()
+            a = partner_of(i, n_dom)
+            pick_both(a)
+            send_both(a)
 
     def turn(begin, end, column_of, at):
         def tile(r, c):
@@ -277,22 +288,29 @@
 
         def pair(a):
             row = flip(a) * n_sub
-            return picked(row + sub, row + sibling, far_proj.at[slot, rows], far_lists.at[slot])
-
-        @pl.loop(0, n_dom - 1)
+            at = pl.ds(pl.multiple_of(a * blk, blk), blk)
+            if c == 0 or slot == 0:
+                hot = hot_of(row + sub, row + sibling, far_lists.at[slot], verts)
+                if slot == 1:
+                    passed_hots[0, :, at] = hot[:, :blk]
+                    passed_hots[1, :, at] = hot[:, blk:]
+            else:
+                hot = jnp.concatenate([passed_hots[0, :, at], passed_hots[1, :, at]], axis=1)
+            return taken(far_proj.at[slot, rows], hot)
+
+        @pl.loop(0, n_dom)
         def _(i):
-            a = turn_of(i, n_dom)
+            a = partner_of(i, n_dom)
             both = pair(a)
             j = base + 2 * a
             out_in[j, rows, :] = both[:, :blk]
             out_in[j + 1, rows, :] = both[:, blk:]
             list_copy(j + 1, plane, a, c, sibling, 1).start()
-            list_copy(j, plane, a, c, sub, 1).start()
-
-        first = pair(0)
-        got_in[plane * n_dom, rows, :] = first[:, :blk]
-        out_in[base + 1, rows, :] = first[:, blk:]
-        list_copy(base + 1, plane, 0, c, sibling, 1).start()
+            pl.when(a != 0)(lambda: list_copy(j, plane, a, c, sub, 1).start())
+
+            @pl.when(a == 0)
+            def _():
+                got_in[plane * n_dom, rows, :] = both[:, :blk]
 
     wide = 2 * blk
 
@@ -335,7 +353,7 @@
             block = jnp.concatenate([got_in[slot, rows, :], got_in[slot + 1, rows, :]], axis=1)
             add_dense(acc_in.at[rows], block, own + slot, 2, False)
 
-    pick_both(n_dom - 1)
+    pick_both(partner_of(0, n_dom))
     pl.semaphore_wait(barrier, peers - 1)
     pl.when(middle)(lambda: send_table(0))
     hand_out_own()
@@ -379,25 +397,44 @@
 
     score(acc_in, inv, bias_col, w_pad, scores, blk)
 
-    def score_copy(k, a, plane):
+    order = [n_dom - 1 - i // 2 - n_dom // 2 * (i % 2) for i in range(n_dom)]
+    order = [a + 1 - 2 * (a % 2) for a in order]
+
+    def score_copy(k, source, a, plane):
         return pltpu.make_async_remote_copy(
-            src_ref=out_sc.at[k], dst_ref=got_sc.at[sub * n_dom + a], send_sem=send_sc, recv_sem=recv_sc.at[sub],
-            device_id=(flip(a), plane), device_id_type=MESH,
-        )
+            src_ref=out_sc.at[k], dst_ref=got_sc.at[source * n_dom + a], send_sem=send_sc,
+            recv_sem=recv_sc.at[source], device_id=(flip(a), plane), device_id_type=MESH,
+        )
+
+    def give(table, hot, base, source, plane, local):
+        lists_for = taken(table, hot)
+        for a in order:
+            one = lists_for[:, a * blk:(a + 1) * blk]
+            out_sc[base + a] = one
+            if a or local is False:
+                score_copy(base + a, source, a, plane).start()
+            elif local is True:
+                got_sc[source * n_dom] = one
+            else:
+                pl.when(jnp.logical_not(local))(lambda: score_copy(base, source, 0, plane).start())
+
+                @pl.when(local)
+                def _():
+                    got_sc[source * n_dom] = one
 
     def deliver(plane):
-        lists_for = taken(scores, hots[plane])
-        for a in [n_dom - 1 - i // 2 - n_dom // 2 * (i % 2) for i in range(n_dom)]:
-            k = plane * n_dom + a
-            out_sc[k] = lists_for[:, a * blk:(a + 1) * blk]
-            if a:
-                score_copy(k, a, plane).start()
-            else:
-                pl.when(sub != plane)(lambda: score_copy(k, 0, plane).start())
-
-        @pl.when(sub == plane)
-        def _():
-            got_sc[sub * n_dom] = lists_for[:, :blk]
+        give(scores, hots[plane], plane * n_dom, sub, plane, sub == plane)
+
+    def table_copy():
+        return pltpu.make_async_remote_copy(
+            src_ref=scores, dst_ref=far_scores, send_sem=table_send, recv_sem=table_recv,
+            device_id=(dom, near), device_id_type=MESH,
+        )
+
+    def pass_scores():
+        table_copy().wait_recv()
+        give(far_scores, passed_hots[1], peers, 0, sibling, False)
+        give(far_scores, passed_hots[0], peers + n_dom, 0, sub, True)
 
     def scores_wait(at, count, plane):
         return pltpu.make_async_remote_copy(
@@ -405,21 +442,32 @@
             recv_sem=recv_sc.at[plane], device_id=(dom, sibling), device_id_type=MESH,
         )
 
+    def scores_sent(count):
+        pltpu.make_async_remote_copy(
+            src_ref=out_sc.at[pl.ds(0, count)], dst_ref=out_sc.at[pl.ds(0, count)], send_sem=send_sc,
+            recv_sem=recv_sc.at[0], device_id=(dom, sibling), device_id_type=MESH,
+        ).wait_send()
+
     def gather(plane):
         slot = plane * n_dom
-        pl.when(plane != sub)(lambda: scores_wait(slot, n_dom, plane).wait_recv())
-        pl.when(plane == sub)(lambda: scores_wait(slot + 1, n_dom - 1, plane).wait_recv())
+        local = jnp.logical_or(plane == sub, jnp.logical_and(plane == 0, sub == 2))
+        pl.when(jnp.logical_not(local))(lambda: scores_wait(slot, n_dom, plane).wait_recv())
+        pl.when(local)(lambda: scores_wait(slot + 1, n_dom - 1, plane).wait_recv())
         block = jnp.concatenate([got_sc[slot + a] for a in range(n_dom)], axis=1)
         add_dense(acc_sc, block, own + slot, n_dom, False)
 
     @pl.when(middle)
     def _():
-        for plane in (sub, near, sibling):
+        for plane in (near, far, sibling, sub):
             deliver(plane)
-        await_sent(1, 2 * (per_step - 1))
-        deliver(far)
-
-    @pl.when(edge)
+
+    @pl.when(sub == 0)
+    def _():
+        table_copy().start()
+        for plane in (sub, sibling):
+            deliver(plane)
+
+    @pl.when(sub == 3)
     def _():
         for plane in (far, sub, near, sibling):
             deliver(plane)
@@ -427,12 +475,22 @@
     add_own(scores, acc_sc)
     await_sent(0, per_step - 1)
     pl.when(edge)(await_table)
+    pl.when(middle)(lambda: await_sent(1, 2 * (per_step - 1)))
     gather(sibling + mid * (sub - sibling))
     gather(near)
-    gather(sub + mid * (sibling - sub))
-    gather(far)
+    pl.when(sub == 2)(pass_scores)
+    last = lax.div(sub, 3)
+    gather(3 * last)
+    gather(3 - 3 * last)
     out[...] = inv * acc_sc[0:classes, :]
-    scores_wait(0, peers - 1, 0).wait_send()
+
+    @pl.when(sub == 0)
+    def _():
+        table_copy().wait_send()
+        scores_sent(2 * n_dom - 1)
+
+    pl.when(lax.rem(sub, 2) == 1)(lambda: scores_sent(peers - 1))
+    pl.when(sub == 2)(lambda: scores_sent(peers + 2 * n_dom - 2))
 
 
 def direct_kernel(n_dom, n_sub, *refs):
@@ -557,7 +615,7 @@
             pltpu.VMEM((hid, verts), f32),
             pltpu.VMEM((padded, hid), bf16),
             pltpu.VMEM((padded, verts), bf16),
-            pltpu.VMEM((peers, padded, blk), bf16),
+            pltpu.VMEM((peers + 2 * n_dom if relay else peers, padded, blk), bf16),
             pltpu.VMEM((peers, padded, blk), bf16),
             pltpu.VMEM((padded, verts), f32),
             pltpu.VMEM(tiles.shape, bf16),
@@ -578,6 +636,10 @@
                 pltpu.VMEM((columns, blk, verts), bf16),
                 pltpu.VMEM((n_sub, verts, n_dom * blk), bf16),
                 pltpu.SemaphoreType.REGULAR,
+                pltpu.VMEM((2, verts, n_dom * blk), bf16),
+                pltpu.VMEM((padded, verts), bf16),
+                pltpu.SemaphoreType.DMA,
+                pltpu.SemaphoreType.DMA,
             ]
             if relay
             else []

time: 52.2 us -> 51.9 us (level)
  Pallas kernels: 51.2 us -> 50.6 us
    pallas_call x1, Pallas kernels: 51.2 us -> 50.6 us  [on_device(): pl.pallas_call(functools.partial(relay_kernel if relay else direct_kernel...]
where the time goes in v3:
time: 51.9 us; the launch traced here: 51.3 us
  Pallas kernels  50.6 us (97%)
  other arithmetic  0.76 us (1%)
    pallas_call x1, Pallas kernels, on_device(): pl.pallas_call(functools.partial(relay_kernel if relay else direct_kernel...  50.6 us

profile of v3, /device:TPU:0, one launch (start us, length us, event | category | flops | bytes accessed | tf_op | source)
XLA Modules:
  0.0 51.3 jit_solution(8863376575442060623)
XLA Ops:
  0.0 0.0 copy-start
  0.0 50.6 %shard_map.91 = f32[41,1024]{1,0:T(8,128)S(1)} custom-call(bf16[602,1024]{1,0:T(8,128)(2,1)} %bitcast.7, bf16[602,256]{1,0:T(8,128)(2,1)} %refs_1_.1, f32[1,256]{1,0:T(1,128)} %bitcast.11, bf16[41,256]{1,0:T(8,128)(2,1)} %bitcast.8, s32[1,1024]{1,0:T(1,128)} %bitcast.10, s32[32,128]{1,0:T(8,128)} %bitcast.9, s32[8,32]{1,0:T(8,128)} %refs_6_.1, ...), custom_call_target="tpu_custom_call" | custom-call | tf_op jit(solution)/shard_map/pallas_call | solution.py:601
  50.6 0.0 copy-done
  50.6 0.8 %add_bitcast_fusion = f32[1024,41]{0,1:T(8,128)} fusion(f32[41,1024]{1,0:T(8,128)S(1)} %shard_map.91, f32[41]{0:T(128)S(1)} %copy-done), kind=kLoop, calls=%fused_computation | loop fusion | flops 41984 | bytes 336036 | tf_op jit(solution)/shard_map/add | solution.py:651
Async XLA Ops:
  0.0 50.6 %copy-start = (f32[41]{0:T(128)S(1)}, f32[41]{0:T(128)}, u32[]{:S(2)}) copy-start(f32[41]{0:T(128)} %param.13) | copy-start | bytes 496

commit v4 on v3

--- a/solution.py
+++ b/solution.py
@@ -66,10 +66,11 @@
         acc[:, span] = term if fresh else acc[:, span] + term
 
 
-def prologue(place, hbm, staged, tiles_hbm, tiles, tile_sem, stage_sem, found, where_tile, found_sem, proj, greet):
-    ft, w_inner, _, _, degrees, _, tile_col = staged
+def prologue(place, hbm, staged, tiles_hbm, tiles, tile_sem, stage_sem, proj, greet):
+    ft, w_inner, _, _, degrees, _, _ = staged
     verts = proj.shape[1]
     part = verts // PARTS
+    whole = ft.shape[0] // 256 * 256
     small = [
         pltpu.make_async_copy(src, dst, stage_sem.at[i])
         for i, (src, dst) in enumerate(zip(hbm, staged))
@@ -98,12 +99,18 @@
     for v in range(PARTS):
         span = slice(v * part, (v + 1) * part)
         wide[v].wait()
-        term = jnp.dot(w_t, ft[:, span], preferred_element_type=jnp.float32)
+        term = jnp.dot(w_t[:, :whole], ft[:whole, span], preferred_element_type=jnp.float32)
+        if whole < ft.shape[0]:
+            term += jnp.dot(w_t[:, whole:], ft[whole:, span], preferred_element_type=jnp.float32)
         if v == PARTS - 1:
             tile_copy.start()
         proj[:, span] = (term * inv[:, span]).astype(proj.dtype)
     for i in (1, 2, 4, 5):
         small[i].wait()
+    return inv, tile_copy
+
+
+def place_tiles(tile_col, found, where_tile, found_sem):
     cols = tile_col[...]
     lane = lax.broadcasted_iota(jnp.int32, found.shape, 1)
     at = jnp.full(found.shape, -1, jnp.int32)
@@ -112,7 +119,7 @@
     found[...] = at
     found_copy = pltpu.make_async_copy(found, where_tile, found_sem)
     found_copy.start()
-    return inv, tile_copy, found_copy
+    return found_copy
 
 
 def turn_of(i, count):
@@ -166,9 +173,7 @@
             for to_dom in doms[step // n_sub:]:
                 pl.semaphore_signal(barrier, inc=1, device_id=(to_dom, to_sub), device_id_type=MESH)
 
-    inv, tile_copy, found_copy = prologue(
-        place, hbm, staged, tiles_hbm, tiles, tile_sem, stage_sem, found, where_tile, found_sem, proj, greet
-    )
+    inv, tile_copy = prologue(place, hbm, staged, tiles_hbm, tiles, tile_sem, stage_sem, proj, greet)
 
     def lists_copy(slot):
         return pltpu.make_async_remote_copy(
@@ -195,24 +200,24 @@
             device_id=(dom, near), device_id_type=MESH,
         ).wait_send()
 
-    def came_in(plane, m, c):
-        return recv_in.at[(n_sub * pairs + lax.rem(plane, 2) * pairs if c else plane * pairs) + m]
+    def came_in(plane, m, c, slot):
+        return recv_in.at[lax.rem(plane, 2) if c is None else 2 + HALVES * slot + c + (m if slot and c else 0)]
 
     def lists_of(ref, at, c):
         return ref.at[at] if c is None else ref.at[at, pl.ds(c * part, part)]
 
-    def list_copy(j, plane, a, c, to_sub, relayed):
+    def list_copy(j, plane, a, c, to_sub, slot=None):
         return pltpu.make_async_remote_copy(
             src_ref=lists_of(out_in, j, c), dst_ref=lists_of(got_in, plane * n_dom + a, c),
-            send_sem=send_in.at[relayed], recv_sem=came_in(plane, lax.div(a, 2), c),
+            send_sem=send_in.at[0 if slot is None else 1], recv_sem=came_in(plane, lax.div(a, 2), c, slot),
             device_id=(flip(a), to_sub), device_id_type=MESH,
         )
 
-    def await_lists(plane, m, c, count=2):
-        at = pl.ds(plane * n_dom + 2 * m + 2 - count, count)
+    def await_lists(plane, a, count, c, slot=None):
         pltpu.make_async_remote_copy(
-            src_ref=lists_of(out_in, pl.ds(0, count), c), dst_ref=lists_of(got_in, at, c),
-            send_sem=send_in.at[0], recv_sem=came_in(plane, m, c),
+            src_ref=lists_of(out_in, pl.ds(0, count), c),
+            dst_ref=lists_of(got_in, pl.ds(plane * n_dom + a, count), c),
+            send_sem=send_in.at[0], recv_sem=came_in(plane, lax.div(a, 2), c, slot),
             device_id=(dom, sibling), device_id_type=MESH,
         ).wait_recv()
 
@@ -245,8 +250,8 @@
             got_in[sub * n_dom] = mine
 
     def send_both(a):
-        list_copy(2 * a + 1, sub, a, None, sibling, 0).start()
-        pl.when(a != 0)(lambda: list_copy(2 * a, sub, a, None, sub, 0).start())
+        list_copy(2 * a + 1, sub, a, None, sibling).start()
+        pl.when(a != 0)(lambda: list_copy(2 * a, sub, a, None, sub).start())
 
     def hand_out_own():
         send_both(partner_of(0, n_dom))
@@ -289,13 +294,12 @@
         def pair(a):
             row = flip(a) * n_sub
             at = pl.ds(pl.multiple_of(a * blk, blk), blk)
-            if c == 0 or slot == 0:
+            if c == 0:
                 hot = hot_of(row + sub, row + sibling, far_lists.at[slot], verts)
-                if slot == 1:
-                    passed_hots[0, :, at] = hot[:, :blk]
-                    passed_hots[1, :, at] = hot[:, blk:]
+                passed_hots[slot, 0, :, at] = hot[:, :blk]
+                passed_hots[slot, 1, :, at] = hot[:, blk:]
             else:
-                hot = jnp.concatenate([passed_hots[0, :, at], passed_hots[1, :, at]], axis=1)
+                hot = jnp.concatenate([passed_hots[slot, 0, :, at], passed_hots[slot, 1, :, at]], axis=1)
             return taken(far_proj.at[slot, rows], hot)
 
         @pl.loop(0, n_dom)
@@ -305,16 +309,15 @@
             j = base + 2 * a
             out_in[j, rows, :] = both[:, :blk]
             out_in[j + 1, rows, :] = both[:, blk:]
-            list_copy(j + 1, plane, a, c, sibling, 1).start()
-            pl.when(a != 0)(lambda: list_copy(j, plane, a, c, sub, 1).start())
+            list_copy(j + 1, plane, a, c, sibling, slot).start()
+            pl.when(a != 0)(lambda: list_copy(j, plane, a, c, sub, slot).start())
 
             @pl.when(a == 0)
             def _():
                 got_in[plane * n_dom, rows, :] = both[:, :blk]
 
-    wide = 2 * blk
-
     def add_dense(acc, block, first, count, fresh):
+        wide = 2 * blk if acc.shape[0] >= part else 8 * blk
         for v in range(0, verts, wide):
             span = slice(v, v + wide)
             weights = dense[pl.ds(first, count), :, span].reshape(count * blk, wide)
@@ -328,35 +331,43 @@
         slot = plane * n_dom + 2 * m
         add_dense(acc_in, jnp.concatenate([got_in[slot], got_in[slot + 1]], axis=1), own + slot, 2, False)
 
-    def add_plane(plane, halves, local):
-        parts = range(HALVES) if halves else (None,)
-
-        @pl.loop(0, pairs - 1)
+    def add_pairs(plane):
+        @pl.loop(0, pairs)
         def _(i):
-            m = turn_of(i, pairs)
-            for c in parts:
-                await_lists(plane, m, c)
-            add_pair(plane, m)
-
-        for c in parts:
-            await_lists(plane, 0, c, 1 if local else 2)
-        add_pair(plane, 0)
-
-    def add_halves(plane, c):
+            add_pair(plane, turn_of(i, pairs))
+
+    def add_plane(plane, local):
+        await_lists(plane, local, n_dom - local, None)
+        add_pairs(plane)
+
+    def add_passed(slot, plane):
+        await_lists(plane, 1, n_dom - 1, 0, slot)
+        if slot:
+            for m in range(pairs):
+                await_lists(plane, 2 * m if m else 1, 2 if m else 1, 1, slot)
+        else:
+            await_lists(plane, 1, n_dom - 1, 1, slot)
+        add_pairs(plane)
+
+    def add_halves(slot, plane, c):
         rows = slice(c * part, (c + 1) * part)
+        if not (slot and c):
+            await_lists(plane, 0, n_dom, c, slot)
 
         @pl.loop(0, pairs)
         def _(i):
             m = turn_of(i, pairs)
-            slot = plane * n_dom + 2 * m
-            await_lists(plane, m, c)
-            block = jnp.concatenate([got_in[slot, rows, :], got_in[slot + 1, rows, :]], axis=1)
-            add_dense(acc_in.at[rows], block, own + slot, 2, False)
+            at = plane * n_dom + 2 * m
+            if slot and c:
+                await_lists(plane, 2 * m, 2, c, slot)
+            block = jnp.concatenate([got_in[at, rows, :], got_in[at + 1, rows, :]], axis=1)
+            add_dense(acc_in.at[rows], block, own + at, 2, False)
 
     pick_both(partner_of(0, n_dom))
     pl.semaphore_wait(barrier, peers - 1)
     pl.when(middle)(lambda: send_table(0))
     hand_out_own()
+    found_copy = place_tiles(staged[6], found, where_tile, found_sem)
     w_pad[...] = jnp.zeros_like(w_pad)
     w_pad[0:classes, :] = w_outer[...]
     bias_col = jnp.broadcast_to(bias[...], (blk, hid)).T
@@ -375,12 +386,12 @@
         turn_slots(2 * n_dom, peers)
         relay(0, 1, near)
         add_own(proj, acc_in)
-        add_plane(sub, False, True)
+        add_plane(sub, 1)
         relay(1, 0, far)
-        add_plane(sibling, False, False)
+        add_plane(sibling, 0)
         relay(1, 1, far)
-        add_plane(near, True, True)
-        add_plane(far, True, True)
+        add_passed(0, near)
+        add_passed(1, far)
 
     @pl.when(edge)
     def _():
@@ -388,12 +399,12 @@
         add_own(proj, acc_in)
         pl.semaphore_wait(clear, 1)
         send_table(1)
-        add_plane(sub, False, True)
-        add_plane(sibling, False, False)
-        add_halves(near, 0)
-        add_halves(near, 1)
-        add_halves(far, 0)
-        add_halves(far, 1)
+        add_plane(sub, 1)
+        add_plane(sibling, 0)
+        add_halves(0, near, 0)
+        add_halves(0, near, 1)
+        add_halves(1, far, 0)
+        add_halves(1, far, 1)
 
     score(acc_in, inv, bias_col, w_pad, scores, blk)
 
@@ -425,16 +436,19 @@
     def deliver(plane):
         give(scores, hots[plane], plane * n_dom, sub, plane, sub == plane)
 
-    def table_copy():
+    def table_copy(slot):
         return pltpu.make_async_remote_copy(
-            src_ref=scores, dst_ref=far_scores, send_sem=table_send, recv_sem=table_recv,
+            src_ref=scores, dst_ref=far_scores.at[slot], send_sem=table_send, recv_sem=table_recv.at[slot],
             device_id=(dom, near), device_id_type=MESH,
         )
 
-    def pass_scores():
-        table_copy().wait_recv()
-        give(far_scores, passed_hots[1], peers, 0, sibling, False)
-        give(far_scores, passed_hots[0], peers + n_dom, 0, sub, True)
+    def pass_scores(slot, source, to_own, to_sibling):
+        table_copy(slot).wait_recv()
+        for own_plane in (slot == 1, slot == 0):
+            if own_plane:
+                give(far_scores.at[slot], passed_hots[slot, 0], to_own, source, sub, True)
+            else:
+                give(far_scores.at[slot], passed_hots[slot, 1], to_sibling, source, sibling, False)
 
     def scores_wait(at, count, plane):
         return pltpu.make_async_remote_copy(
@@ -450,7 +464,8 @@
 
     def gather(plane):
         slot = plane * n_dom
-        local = jnp.logical_or(plane == sub, jnp.logical_and(plane == 0, sub == 2))
+        passed = jnp.logical_or(plane == near, jnp.logical_and(plane == 0, sub == 2))
+        local = jnp.logical_or(plane == sub, jnp.logical_and(middle, passed))
         pl.when(jnp.logical_not(local))(lambda: scores_wait(slot, n_dom, plane).wait_recv())
         pl.when(local)(lambda: scores_wait(slot + 1, n_dom - 1, plane).wait_recv())
         block = jnp.concatenate([got_sc[slot + a] for a in range(n_dom)], axis=1)
@@ -458,14 +473,14 @@
 
     @pl.when(middle)
     def _():
-        for plane in (near, far, sibling, sub):
+        table_copy(0).start()
+        for plane in (sibling, sub):
             deliver(plane)
 
     @pl.when(sub == 0)
     def _():
-        table_copy().start()
-        for plane in (sub, sibling):
-            deliver(plane)
+        table_copy(1).start()
+        deliver(sub)
 
     @pl.when(sub == 3)
     def _():
@@ -475,22 +490,31 @@
     add_own(scores, acc_sc)
     await_sent(0, per_step - 1)
     pl.when(edge)(await_table)
+    pl.when(middle)(lambda: pass_scores(0, near, near * n_dom, far * n_dom))
     pl.when(middle)(lambda: await_sent(1, 2 * (per_step - 1)))
-    gather(sibling + mid * (sub - sibling))
-    gather(near)
-    pl.when(sub == 2)(pass_scores)
-    last = lax.div(sub, 3)
-    gather(3 * last)
-    gather(3 - 3 * last)
+    pl.when(sub == 0)(lambda: deliver(sibling))
+    on = [lax.div(3 - sub, 3), 0, 0, lax.div(sub, 3)]
+    on[1] = lax.rem(sub, 2) - on[3]
+    on[2] = 1 - on[0] - on[1] - on[3]
+    first, second, third, fourth = (
+        sum(here * plane for here, plane in zip(on, planes))
+        for planes in ((0, 1, 2, 2), (3, 2, 1, 1), (1, 0, 3, 3), (2, 3, 0, 0))
+    )
+    gather(first)
+    pl.when(sub == 2)(lambda: pass_scores(1, 0, peers, peers + n_dom))
+    gather(second)
+    gather(third)
+    gather(fourth)
     out[...] = inv * acc_sc[0:classes, :]
 
     @pl.when(sub == 0)
     def _():
-        table_copy().wait_send()
         scores_sent(2 * n_dom - 1)
 
-    pl.when(lax.rem(sub, 2) == 1)(lambda: scores_sent(peers - 1))
-    pl.when(sub == 2)(lambda: scores_sent(peers + 2 * n_dom - 2))
+    pl.when(sub == 1)(lambda: scores_sent(peers - 2))
+    pl.when(sub == 2)(lambda: scores_sent(peers + 2 * n_dom - 3))
+    pl.when(sub == 3)(lambda: scores_sent(peers - 1))
+    pl.when(sub != 3)(lambda: table_copy(0).wait_send())
 
 
 def direct_kernel(n_dom, n_sub, *refs):
@@ -514,9 +538,7 @@
         def _(k):
             pl.semaphore_signal(barrier, inc=1, device_id=place.target(k), device_id_type=MESH)
 
-    inv, tile_copy, found_copy = prologue(
-        place, hbm, staged, tiles_hbm, tiles, tile_sem, stage_sem, found, where_tile, found_sem, proj, greet
-    )
+    inv, tile_copy = prologue(place, hbm, staged, tiles_hbm, tiles, tile_sem, stage_sem, proj, greet)
     pl.semaphore_wait(barrier, peers - 1)
 
     def copy(src, dst, sends, recvs, k):
@@ -563,6 +585,7 @@
             arrived(k)
 
     deliver(proj, out_in, got_in, send_in, recv_in)
+    found_copy = place_tiles(staged[6], found, where_tile, found_sem)
     w_pad[...] = jnp.zeros_like(w_pad)
     w_pad[0:classes, :] = w_outer[...]
     bias_col = jnp.broadcast_to(bias[...], (blk, hid)).T
@@ -621,7 +644,7 @@
             pltpu.VMEM(tiles.shape, bf16),
             pltpu.SemaphoreType.DMA,
             pltpu.SemaphoreType.DMA((2 if relay else peers,)),
-            pltpu.SemaphoreType.DMA(((n_sub + 2) * n_dom // 2 if relay else peers,)),
+            pltpu.SemaphoreType.DMA((1 + 2 * HALVES + n_dom // 2 if relay else peers,)),
             pltpu.SemaphoreType.DMA if relay else pltpu.SemaphoreType.DMA((peers,)),
             pltpu.SemaphoreType.DMA((n_sub if relay else peers,)),
         ]
@@ -636,10 +659,10 @@
                 pltpu.VMEM((columns, blk, verts), bf16),
                 pltpu.VMEM((n_sub, verts, n_dom * blk), bf16),
                 pltpu.SemaphoreType.REGULAR,
-                pltpu.VMEM((2, verts, n_dom * blk), bf16),
-                pltpu.VMEM((padded, verts), bf16),
+                pltpu.VMEM((2, 2, verts, n_dom * blk), bf16),
+                pltpu.VMEM((2, padded, verts), bf16),
                 pltpu.SemaphoreType.DMA,
-                pltpu.SemaphoreType.DMA,
+                pltpu.SemaphoreType.DMA((2,)),
             ]
             if relay
             else []

time: 51.9 us -> 51.7 us (level)
  no operation moved by 1% of the time
where the time goes in v4:
time: 51.7 us; the launch traced here: 51.6 us
  Pallas kernels  50.8 us (98%)
  other arithmetic  0.76 us (1%)
    pallas_call x1, Pallas kernels, on_device(): pl.pallas_call(functools.partial(relay_kernel if relay else direct_kernel...  50.8 us

profile of v4, /device:TPU:0, one launch (start us, length us, event | category | flops | bytes accessed | tf_op | source)
XLA Modules:
  0.0 51.6 jit_solution(5028907828794830001)
XLA Ops:
  0.0 0.0 copy-start
  0.0 50.8 %shard_map.91 = f32[41,1024]{1,0:T(8,128)S(1)} custom-call(bf16[602,1024]{1,0:T(8,128)(2,1)} %bitcast.7, bf16[602,256]{1,0:T(8,128)(2,1)} %refs_1_.1, f32[1,256]{1,0:T(1,128)} %bitcast.11, bf16[41,256]{1,0:T(8,128)(2,1)} %bitcast.8, s32[1,1024]{1,0:T(1,128)} %bitcast.10, s32[32,128]{1,0:T(8,128)} %bitcast.9, s32[8,32]{1,0:T(8,128)} %refs_6_.1, ...), custom_call_target="tpu_custom_call" | custom-call | tf_op jit(solution)/shard_map/pallas_call | solution.py:624
  50.8 0.0 copy-done
  50.8 0.8 %add_bitcast_fusion = f32[1024,41]{0,1:T(8,128)} fusion(f32[41,1024]{1,0:T(8,128)S(1)} %shard_map.91, f32[41]{0:T(128)S(1)} %copy-done), kind=kLoop, calls=%fused_computation | loop fusion | flops 41984 | bytes 336036 | tf_op jit(solution)/shard_map/add | solution.py:674
Async XLA Ops:
  0.0 50.8 %copy-start = (f32[41]{0:T(128)S(1)}, f32[41]{0:T(128)}, u32[]{:S(2)}) copy-start(f32[41]{0:T(128)} %param.13) | copy-start | bytes 496

commit v5 on v4

--- a/solution.py
+++ b/solution.py
@@ -370,7 +370,7 @@
     found_copy = place_tiles(staged[6], found, where_tile, found_sem)
     w_pad[...] = jnp.zeros_like(w_pad)
     w_pad[0:classes, :] = w_outer[...]
-    bias_col = jnp.broadcast_to(bias[...], (blk, hid)).T
+    bias_col = jnp.broadcast_to(bias[...], (2 * blk, hid)).T
     tile_copy.wait()
     found_copy.wait()
     turn(0, own, lambda i: i, 0)
@@ -406,7 +406,7 @@
         add_halves(1, far, 0)
         add_halves(1, far, 1)
 
-    score(acc_in, inv, bias_col, w_pad, scores, blk)
+    score(acc_in, inv, bias_col, w_pad, scores, 2 * blk)
 
     order = [n_dom - 1 - i // 2 - n_dom // 2 * (i % 2) for i in range(n_dom)]
     order = [a + 1 - 2 * (a % 2) for a in order]
@@ -417,10 +417,16 @@
             recv_sem=recv_sc.at[source], device_id=(flip(a), plane), device_id_type=MESH,
         )
 
-    def give(table, hot, base, source, plane, local):
-        lists_for = taken(table, hot)
-        for a in order:
-            one = lists_for[:, a * blk:(a + 1) * blk]
+    def give(table, hot_all, base, source, plane, local, pieces=n_dom):
+        for i, a in enumerate(order):
+            if i % pieces == 0:
+                these = order[i:i + pieces]
+                hot = hot_all[...] if pieces == n_dom else jnp.concatenate(
+                    [hot_all[:, b * blk:(b + 1) * blk] for b in these], axis=1
+                )
+                lists_for = taken(table, hot)
+            at = a if pieces == n_dom else i % pieces
+            one = lists_for[:, at * blk:(at + 1) * blk]
             out_sc[base + a] = one
             if a or local is False:
                 score_copy(base + a, source, a, plane).start()
@@ -433,8 +439,8 @@
                 def _():
                     got_sc[source * n_dom] = one
 
-    def deliver(plane):
-        give(scores, hots[plane], plane * n_dom, sub, plane, sub == plane)
+    def deliver(plane, pieces=n_dom):
+        give(scores, hots.at[plane], plane * n_dom, sub, plane, sub == plane, pieces)
 
     def table_copy(slot):
         return pltpu.make_async_remote_copy(
@@ -444,11 +450,8 @@
 
     def pass_scores(slot, source, to_own, to_sibling):
         table_copy(slot).wait_recv()
-        for own_plane in (slot == 1, slot == 0):
-            if own_plane:
-                give(far_scores.at[slot], passed_hots[slot, 0], to_own, source, sub, True)
-            else:
-                give(far_scores.at[slot], passed_hots[slot, 1], to_sibling, source, sibling, False)
+        give(far_scores.at[slot], passed_hots.at[slot, 1], to_sibling, source, sibling, False)
+        give(far_scores.at[slot], passed_hots.at[slot, 0], to_own, source, sub, True)
 
     def scores_wait(at, count, plane):
         return pltpu.make_async_remote_copy(
@@ -484,7 +487,8 @@
 
     @pl.when(sub == 3)
     def _():
-        for plane in (far, sub, near, sibling):
+        deliver(far, n_dom // 2)
+        for plane in (sub, near, sibling):
             deliver(plane)
 
     add_own(scores, acc_sc)
@@ -588,11 +592,11 @@
     found_copy = place_tiles(staged[6], found, where_tile, found_sem)
     w_pad[...] = jnp.zeros_like(w_pad)
     w_pad[0:classes, :] = w_outer[...]
-    bias_col = jnp.broadcast_to(bias[...], (blk, hid)).T
+    bias_col = jnp.broadcast_to(bias[...], (2 * blk, hid)).T
     tile_copy.wait()
     found_copy.wait()
     aggregate(proj, out_in, got_in, send_in, recv_in, acc_in)
-    score(acc_in, inv, bias_col, w_pad, scores, blk)
+    score(acc_in, inv, bias_col, w_pad, scores, 2 * blk)
     deliver(scores, out_sc, got_sc, send_sc, recv_sc)
     aggregate(scores, out_sc, got_sc, send_sc, recv_sc, acc_sc)
     out[...] = inv * acc_sc[0:classes, :]

time: 51.7 us -> 51.7 us (level)
  no operation moved by 1% of the time
where the time goes in v5:
time: 51.7 us; the launch traced here: 51.6 us
  Pallas kernels  50.8 us (98%)
  other arithmetic  0.76 us (1%)
    pallas_call x1, Pallas kernels, on_device(): pl.pallas_call(functools.partial(relay_kernel if relay else direct_kernel...  50.8 us

profile of v5, /device:TPU:0, one launch (start us, length us, event | category | flops | bytes accessed | tf_op | source)
XLA Modules:
  0.0 51.6 jit_solution(10763951163729269042)
XLA Ops:
  0.0 0.0 copy-start
  0.0 50.8 %shard_map.91 = f32[41,1024]{1,0:T(8,128)S(1)} custom-call(bf16[602,1024]{1,0:T(8,128)(2,1)} %bitcast.7, bf16[602,256]{1,0:T(8,128)(2,1)} %refs_1_.1, f32[1,256]{1,0:T(1,128)} %bitcast.11, bf16[41,256]{1,0:T(8,128)(2,1)} %bitcast.8, s32[1,1024]{1,0:T(1,128)} %bitcast.10, s32[32,128]{1,0:T(8,128)} %bitcast.9, s32[8,32]{1,0:T(8,128)} %refs_6_.1, ...), custom_call_target="tpu_custom_call" | custom-call | tf_op jit(solution)/shard_map/pallas_call | solution.py:628
  50.8 0.0 copy-done
  50.8 0.8 %add_bitcast_fusion = f32[1024,41]{0,1:T(8,128)} fusion(f32[41,1024]{1,0:T(8,128)S(1)} %shard_map.91, f32[41]{0:T(128)S(1)} %copy-done), kind=kLoop, calls=%fused_computation | loop fusion | flops 41984 | bytes 336036 | tf_op jit(solution)/shard_map/add | solution.py:678
Async XLA Ops:
  0.0 50.8 %copy-start = (f32[41]{0:T(128)S(1)}, f32[41]{0:T(128)}, u32[]{:S(2)}) copy-start(f32[41]{0:T(128)} %param.13) | copy-start | bytes 496
